TPU v7x, 32 devices: a whole 2x2x4 slice. The times are simulated.
32 devices in a mesh: lon: 2 (over x), lat: 4 (over y, core), mem: 4 (over z).
Axes of the slice: x: 2, y: 2, z: 4, core: 2. Of those that a mesh axis runs over, the one named last changes fastest.
Arguments:
- anomalies: bfloat16 [32, 4, 128, 512], P('mem', None, 'lon', 'lat'), may hold values from -6 to 6
- spread: float32 [4, 128, 512], P(None, 'lon', 'lat'), may hold values from 0.5 to 2
- obs_index: int32 [2, 4, 2048], P('lon', 'lat'), may hold values from 0 to 32767
- innovation: float32 [2, 4, 2048], P('lon', 'lat'), may hold values from -6 to 6
- obs_weight: float32 [2, 4, 2048], P('lon', 'lat'), may hold values from 0.5 to 8
- band_width: int32 [2, 4], replicated, may hold values from 6 to 12, as said below
Outputs:
- control_ens: float32 [32, 4, 128, 512], P('mem', None, 'lon', 'lat')
- control_static: float32 [4, 128, 512], P(None, 'lon', 'lat')
Inputs may be any that keep to these rules, and one draw needn't show every extreme that they name: `obs_index`: A cell of the tile's 4 x 64 x 128 block, flattened with latitude fastest. `band_width`: in each of the two rows some level has exactly 12.
All inputs are finite; a program needn't handle non-finite values.
Results may differ from a plain program's by a relative error of at most 0.0003.
Values may be sent and summed in bfloat16 or wider, within the bound.
A program may use at most 64 MiB of HBM per device.

v0:
```python
import math

import jax
import jax.numpy as jnp
from jax import lax
from jax.sharding import PartitionSpec as P

BAND = 12
ITERS = 2


hybrid_ens = 0.75
hybrid_static = 0.25


def with_halo(block, sides, width, periodic):
    for axis, dim in sides:
        count = lax.axis_size(axis)
        forward = [(i, i + 1) for i in range(count - 1)]
        if periodic:
            forward.append((count - 1, 0))
        backward = [(target, source) for source, target in forward]
        low = lax.ppermute(
            lax.slice_in_dim(block, block.shape[dim] - width, None, axis=dim), axis, forward
        )
        high = lax.ppermute(lax.slice_in_dim(block, 0, width, axis=dim), axis, backward)
        block = jnp.concatenate([low, block, high], axis=dim)
    return block


def band_table(band_width):
    offsets = jnp.arange(-BAND, BAND + 1).astype(jnp.float32)
    widths = band_width.astype(jnp.float32)[..., None]
    shape_raw = jnp.exp(-0.5 * (offsets / (0.5 * widths)) ** 2)
    shape_raw = jnp.where(jnp.abs(offsets) <= widths, shape_raw, 0.0)
    return shape_raw / jnp.sum(shape_raw, axis=-1, keepdims=True)


def band_matrix(band_weights, cells):
    rows_iota = jnp.arange(cells, dtype=jnp.int32)[:, None]
    cols_iota = jnp.arange(cells + 2 * BAND, dtype=jnp.int32)[None, :]
    shifts = jnp.arange(2 * BAND + 1, dtype=jnp.int32)
    onehot = ((cols_iota - rows_iota)[:, :, None] == shifts).astype(jnp.float32)
    return jnp.einsum("ls,ijs->lij", band_weights, onehot, precision=lax.Precision.HIGHEST)


def per_device(anomalies, spread, obs_index, innovation, obs_weight, band_width):
    members = anomalies.shape[0]
    levels, lon_cells, lat_cells = spread.shape
    mem_count = lax.axis_size("mem")
    coef_ens = math.sqrt(hybrid_ens / (members * mem_count))
    coef_static = math.sqrt(hybrid_static)
    band_weights = band_table(band_width)
    lon_matrix = band_matrix(band_weights[0], lon_cells)
    lat_matrix = band_matrix(band_weights[1], lat_cells)
    owner_mask = jnp.where(lax.axis_index("mem") == 0, 1.0, 0.0).astype(jnp.float32)
    field_weight = jnp.concatenate([jnp.ones((members,), jnp.float32), owner_mask[None]])
    obs_flat = obs_index.reshape(-1)
    weights = obs_weight.reshape(-1)
    plane_cells = lon_cells * lat_cells

    def smooth(extended):
        lon_smooth = jnp.einsum(
            "flja,lij->flia", extended, lon_matrix, precision=lax.Precision.HIGHEST
        )
        return jnp.einsum("flia,lka->flik", lon_smooth, lat_matrix, precision=lax.Precision.HIGHEST)

    def observe(field, first_level):
        flat_field = field.reshape(-1)
        cell_count = flat_field.shape[0]
        relative = obs_flat - first_level * plane_cells
        inside = (relative >= 0) & (relative < cell_count)
        clipped = jnp.clip(relative, 0, cell_count - 1)
        obs_term = jnp.where(inside, weights * flat_field[clipped], 0.0)
        return jnp.zeros((cell_count,), jnp.float32).at[clipped].add(obs_term).reshape(field.shape)

    def adjoint(gradient):
        products = jnp.concatenate(
            [
                coef_ens * anomalies.astype(jnp.float32) * gradient[None],
                (coef_static * spread * gradient)[None],
            ],
            axis=0,
        )
        prod_rim = with_halo(products, (("lat", 3),), BAND, False)
        prod_ext = with_halo(prod_rim, (("lon", 2),), BAND, True)
        return smooth(prod_ext)

    def forward(direction):
        dir_rim = with_halo(direction.astype(jnp.bfloat16), (("lat", 3),), BAND, False).astype(
            direction.dtype
        )
        dir_ext = with_halo(dir_rim.astype(jnp.bfloat16), (("lon", 2),), BAND, True).astype(
            dir_rim.dtype
        )
        localized = smooth(dir_ext)
        member_part = coef_ens * jnp.sum(
            anomalies.astype(jnp.float32) * localized[:members], axis=0
        )
        static_part = coef_static * spread * localized[members]
        combined = lax.psum(member_part, "mem") + static_part
        return observe(combined, 0)

    def hessian(direction):
        return direction + adjoint(forward(direction))

    def local_dot(left, right):
        return jnp.sum(jnp.sum(left * right, axis=(1, 2, 3)) * field_weight)

    def two_products(residual, hess_image):
        return lax.psum(
            (local_dot(residual, residual), local_dot(residual, hess_image)), ("lon", "lat", "mem")
        )

    start_grad = (
        jnp.zeros((levels * plane_cells,), jnp.float32)
        .at[obs_flat]
        .add(weights * innovation.reshape(-1))
        .reshape(levels, lon_cells, lat_cells)
    )
    right_side = adjoint(start_grad)
    control = jnp.zeros_like(right_side)
    residual = right_side
    hess_image = hessian(residual)
    norm_now, curve_dot = two_products(residual, hess_image)
    step_size = norm_now / curve_dot
    direction, hess_along = (residual, hess_image)
    for iteration in range(ITERS):
        control = control + step_size * direction
        residual = residual - step_size * hess_along
        if iteration + 1 < ITERS:
            hess_image = hessian(residual)
            norm_next, curve_dot = two_products(residual, hess_image)
            beta_ratio = norm_next / norm_now
            step_size = norm_next / (curve_dot - beta_ratio * norm_next / step_size)
            direction = residual + beta_ratio * direction
            hess_along = hess_image + beta_ratio * hess_along
            norm_now = norm_next
    return (control[:members], control[members])


def solution(mesh):
    return jax.shard_map(
        per_device,
        mesh=mesh,
        in_specs=(
            P("mem", None, "lon", "lat"),
            P(None, "lon", "lat"),
            P("lon", "lat", None),
            P("lon", "lat", None),
            P("lon", "lat", None),
            P(),
        ),
        out_specs=(P("mem", None, "lon", "lat"), P(None, "lon", "lat")),
        check_vma=False,
    )
```

profile of v0, /device:TPU:0, one launch (start us, length us, event | category | flops | bytes accessed | tf_op | source)
XLA Modules:
  0.0 464.0 jit_solution(16515144680246430070)
XLA Ops:
  7.2 1.3 compare_select_fusion
  9.2 11.3 %scatter_custom_fusion = f32[32768]{0:T(1024)S(1)} fusion(s32[2048]{0:T(1024)S(1)} %bitcast.118, f32[2048]{0:T(1024)S(1)} %mul.146, f32[]{:T(128)} %constant.13.clone.1), kind=kCustom, calls=%fused_computation.126 | custom fusion | flops 2048 | bytes 131076 | tf_op jit(solution)/shard_map/scatter-add | solution.py:118
  21.7 1.6 copy.76
  23.6 1.3 collective-permute-start.1
  25.0 3.2 collective-permute-start
  29.6 3.3 fusion.105
  32.9 3.2 copy.86
  36.2 3.0 collective-permute-start.3
  39.2 3.6 copy.85
  43.7 4.1 collective-permute-done.3
  47.8 3.2 copy.88
  51.0 6.4 %collective-permute-done.2 = f32[9,4,12,152]{3,1,2,0:T(4,128)} collective-permute-done((f32[9,4,12,152]{3,1,2,0:T(4,128)}, f32[9,4,12,152]{3,1,2,0:T(4,128)}, u32[]{:S(2)}, u32[]{:S(2)}) %collective-permute-start.2) | collective-permute-done | bytes 262688 | tf_op jit(solution)/shard_map/ppermute | solution.py:23
  57.4 3.2 copy.87
  60.6 9.1 %fusion = f32[4,64,9,152]{3,1,2,0:T(8,128)S(1)} fusion(f32[9,4,12,152]{2,3,0,1:T(8,128)} %copy.88, f32[9,4,64,12]{2,3,0,1:T(8,128)S(1)} %copy.84, f32[1,4,64,128]{2,3,0,1:T(8,128)S(1)} %get-tuple-element.43, f32[9,4,64,12]{2,3,0,1:T(8,128)S(1)} %copy.83, f32[9,4,12,152]{2,3,0,1:T(8,128)} %copy.87, f32[4,64,88,1]{2,0,1,3:T(4,128)S(1)} %convolution_bitcast_fusion.2, ...), kind=kOutput, calls=%fused_computation.11 | convolution fusion | flops 372751616 | bytes 3023872 | tf_op jit(solution)/shard_map/flja,lij->flia/dot_general | solution.py:63
  69.7 3.1 fusion.108
  73.3 1.5 collective-permute-start.5
  75.1 4.8 %collective-permute-start.4 = (bf16[9,4,64,12]{2,1,3,0:T(4,128)(2,1)S(1)}, bf16[9,4,64,12]{2,1,3,0:T(4,128)(2,1)S(1)}, u32[]{:S(2)}, u32[]{:S(2)}) collective-permute-start(bf16[9,4,64,12]{2,1,3,0:T(4,128)(2,1)S(1)} %copy.91), channel_id=1, source_target_pairs={{0,4},{4,8},{8,12},{1,5},{5,9},{9,13},{2,6},{6,10},{10,14},{3,7},{... | collective-permute-start | bytes 165896 | tf_op jit(solution)/shard_map/ppermute | solution.py:23
  81.7 2.1 collective-permute-start.7
  83.8 5.9 %collective-permute-done.7 = bf16[9,4,12,152]{3,2,0,1:T(8,128)(2,1)S(1)} collective-permute-done((bf16[9,4,12,152]{3,2,0,1:T(8,128)(2,1)S(1)}, bf16[9,4,12,152]{3,2,0,1:T(8,128)(2,1)S(1)}, u32[]{:S(2)}, u32[]{:S(2)}) %collective-permute-start.7) | collective-permute-done | bytes 131360 | tf_op jit(solution)/shard_map/ppermute | solution.py:26
  89.8 6.3 %collective-permute-done.6 = bf16[9,4,12,152]{3,2,0,1:T(8,128)(2,1)S(1)} collective-permute-done((bf16[9,4,12,152]{3,2,0,1:T(8,128)(2,1)S(1)}, bf16[9,4,12,152]{3,2,0,1:T(8,128)(2,1)S(1)}, u32[]{:S(2)}, u32[]{:S(2)}) %collective-permute-start.6) | collective-permute-done | bytes 131360 | tf_op jit(solution)/shard_map/ppermute | solution.py:23
  96.1 2.0 convolution_bitcast_fusion.1
  98.1 4.4 fusion.29
  104.3 38.2 %all-reduce.6.cloned.1.call-done = f32[4,64,128]{1,2,0:T(8,128)} async-done(((f32[4,64,128]{1,2,0:T(8,128)}), f32[4,64,128]{1,2,0:T(8,128)}) %all-reduce.6.cloned.1.call-update) | async-done | bytes 131088 | tf_op jit(solution)/shard_map/psum | solution.py:101
  142.5 1.8 fusion.82
  145.3 11.8 %gather_fusion = f32[2048]{0:T(1024)S(1)} fusion(f32[32768]{0:T(1024)S(1)} %bitcast.104, s32[2048]{0:T(1024)S(1)} %broadcast_clamp_fusion), kind=kCustom, calls=%fused_computation | custom fusion | bytes 24576 | tf_op jit(solution)/shard_map/gather | solution.py:74
  157.1 11.4 %scatter_custom_fusion.1 = f32[32768]{0:T(1024)S(1)} fusion(s32[2048]{0:T(1024)} %bitcast.114, f32[2048]{0:T(1024)S(1)} %multiply_select_fusion.1, f32[]{:T(128)} %constant.13.clone.1), kind=kCustom, calls=%fused_computation.124 | custom fusion | flops 2048 | bytes 131584 | tf_op jit(solution)/shard_map/scatter-add | solution.py:75
  169.2 1.3 collective-permute-start.9
  170.6 3.4 collective-permute-start.8
  175.9 3.4 fusion.104
  179.3 3.6 copy.107
  182.9 1.5 collective-permute-start.11
  184.4 3.6 copy.106
  188.6 5.9 %collective-permute-done.11 = f32[9,4,12,152]{3,1,2,0:T(4,128)} collective-permute-done((f32[9,4,12,152]{3,1,2,0:T(4,128)}, f32[9,4,12,152]{3,1,2,0:T(4,128)}, u32[]{:S(2)}, u32[]{:S(2)}) %collective-permute-start.11) | collective-permute-done | bytes 262688 | tf_op jit(solution)/shard_map/ppermute | solution.py:26
  194.4 3.1 copy.109
  197.5 6.4 %collective-permute-done.10 = f32[9,4,12,152]{3,1,2,0:T(4,128)} collective-permute-done((f32[9,4,12,152]{3,1,2,0:T(4,128)}, f32[9,4,12,152]{3,1,2,0:T(4,128)}, u32[]{:S(2)}, u32[]{:S(2)}) %collective-permute-start.10) | collective-permute-done | bytes 262688 | tf_op jit(solution)/shard_map/ppermute | solution.py:23
  203.9 3.2 copy.108
  207.1 9.4 %fusion.14 = f32[4,64,9,152]{3,1,2,0:T(8,128)S(1)} fusion(f32[4,64,88,1]{2,0,1,3:T(4,128)S(1)} %copy-done.17, f32[9,4,12,152]{2,3,1,0:T(8,128)} %copy.109, f32[9,4,64,12]{2,3,1,0:T(8,128)} %copy-done.12, f32[1,4,64,128]{2,3,1,0:T(8,128)S(1)} %get-tuple-element.41, f32[8,4,64,128]{2,3,1,0:T(8,128)S(1)} %convert_multiply_fusion.2, ...), kind=kOutput, calls=%fused_computation.29 | convolution fusion | flops 372227328 | bytes 3417088 | tf_op jit(solution)/shard_map/flja,lij->flia/dot_general | solution.py:63
  216.5 3.1 multiply_reduce_fusion.1
  220.3 41.6 %all-reduce.2 = (f32[]{:T(128)}, f32[]{:T(128)}) all-reduce(f32[]{:T(128)} %get-tuple-element.50, f32[]{:T(128)} %get-tuple-element.49), channel_id=1, replica_groups=mesh['lon'=2,'lat'=4,'mem'=4] {'lon','lat','mem'}, use_global_device_ids=true, to_apply=%region_4.5 | all-reduce | flops 2 | bytes 16 | tf_op jit(solution)/shard_map/psum | solution.py:111
  263.4 2.6 fusion.102
  266.5 1.3 collective-permute-start.13
  268.1 3.2 collective-permute-start.12
  272.9 2.3 collective-permute-start.15
  275.3 7.0 %collective-permute-done.15 = bf16[9,4,12,152]{3,2,0,1:T(8,128)(2,1)S(1)} collective-permute-done((bf16[9,4,12,152]{3,2,0,1:T(8,128)(2,1)S(1)}, bf16[9,4,12,152]{3,2,0,1:T(8,128)(2,1)S(1)}, u32[]{:S(2)}, u32[]{:S(2)}) %collective-permute-start.15) | collective-permute-done | bytes 131360 | tf_op jit(solution)/shard_map/ppermute | solution.py:26
  282.4 6.3 %collective-permute-done.14 = bf16[9,4,12,152]{3,2,0,1:T(8,128)(2,1)S(1)} collective-permute-done((bf16[9,4,12,152]{3,2,0,1:T(8,128)(2,1)S(1)}, bf16[9,4,12,152]{3,2,0,1:T(8,128)(2,1)S(1)}, u32[]{:S(2)}, u32[]{:S(2)}) %collective-permute-start.14) | collective-permute-done | bytes 131360 | tf_op jit(solution)/shard_map/ppermute | solution.py:23
  288.7 2.0 convolution_bitcast_fusion
  290.7 4.4 fusion.32
  296.1 35.5 %all-reduce.8.cloned.1.call-done = f32[4,64,128]{1,2,0:T(8,128)} async-done(((f32[4,64,128]{1,2,0:T(8,128)}), f32[4,64,128]{1,2,0:T(8,128)}) %all-reduce.8.cloned.1.call-update) | async-done | bytes 131088 | tf_op jit(solution)/shard_map/psum | solution.py:101
  331.6 1.8 fusion.80
  334.5 11.8 %gather_fusion.1 = f32[2048]{0:T(1024)S(1)} fusion(f32[32768]{0:T(1024)S(1)} %bitcast.103, s32[2048]{0:T(1024)S(1)} %broadcast_clamp_fusion), kind=kCustom, calls=%fused_computation.1 | custom fusion | bytes 24576 | tf_op jit(solution)/shard_map/gather | solution.py:74
  346.3 11.4 %scatter_custom_fusion.2 = f32[32768]{0:T(1024)S(1)} fusion(s32[2048]{0:T(1024)} %bitcast.115, f32[2048]{0:T(1024)S(1)} %multiply_select_fusion, f32[]{:T(128)} %constant.13.clone.1), kind=kCustom, calls=%fused_computation.122 | custom fusion | flops 2048 | bytes 131584 | tf_op jit(solution)/shard_map/scatter-add | solution.py:75
  358.3 1.3 collective-permute-start.17
  359.7 3.3 collective-permute-start.16
  365.0 3.4 fusion.103
  368.4 3.6 copy.129
  372.0 1.5 collective-permute-start.19
  373.5 3.6 copy.128
  378.5 5.0 %collective-permute-done.19 = f32[9,4,12,152]{3,1,2,0:T(4,128)} collective-permute-done((f32[9,4,12,152]{3,1,2,0:T(4,128)}, f32[9,4,12,152]{3,1,2,0:T(4,128)}, u32[]{:S(2)}, u32[]{:S(2)}) %collective-permute-start.19) | collective-permute-done | bytes 262688 | tf_op jit(solution)/shard_map/ppermute | solution.py:26
  383.5 3.1 copy.131
  386.6 6.4 %collective-permute-done.18 = f32[9,4,12,152]{3,1,2,0:T(4,128)} collective-permute-done((f32[9,4,12,152]{3,1,2,0:T(4,128)}, f32[9,4,12,152]{3,1,2,0:T(4,128)}, u32[]{:S(2)}, u32[]{:S(2)}) %collective-permute-start.18) | collective-permute-done | bytes 262688 | tf_op jit(solution)/shard_map/ppermute | solution.py:23
  393.0 3.2 copy.130
  396.1 9.4 %fusion.12 = f32[4,64,9,152]{3,1,2,0:T(8,128)S(1)} fusion(f32[4,64,88,1]{2,0,1,3:T(4,128)} %copy-done.16, f32[9,4,12,152]{2,3,1,0:T(8,128)} %copy.131, f32[9,4,64,12]{2,3,1,0:T(8,128)} %copy-done.14, f32[1,4,64,128]{2,3,1,0:T(8,128)S(1)} %get-tuple-element.39, f32[8,4,64,128]{2,3,1,0:T(8,128)S(1)} %convert_multiply_fusion, f32[9,4,64,12]{2,3,1,0:T(8,128)} %copy-done.15, ...), kind=kOutput, calls=%fused_computation.27 | convolution fusion | flops 372227328 | bytes 3417088 | tf_op jit(solution)/shard_map/flja,lij->flia/dot_general | solution.py:63
  405.5 2.1 fusion.67
  408.4 41.7 %all-reduce.1 = (f32[]{:T(128)}, f32[]{:T(128)}) all-reduce(f32[]{:T(128)} %multiply_reduce_fusion.4, f32[]{:T(128)} %multiply_reduce_fusion.3), channel_id=1, replica_groups=mesh['lon'=2,'lat'=4,'mem'=4] {'lon','lat','mem'}, use_global_device_ids=true, to_apply=%region_13.14 | all-reduce | flops 2 | bytes 16 | tf_op jit(solution)/shard_map/psum | solution.py:111
  (135 shorter events, 25.2 us)
Async XLA Ops:
  7.2 135.3 %all-reduce.6.cloned.1.call-start = ((), (), s32[]{:S(2)}) async-start(), calls=%async_computation | async-start | bytes 524288 | tf_op jit(solution)/shard_map/psum | solution.py:101
  21.7 1.8 copy-start.4
  23.3 4.9 %copy-start.23 = (s32[2,4]{1,0:T(2,128)S(1)}, s32[2,4]{1,0:T(2,128)}, u32[]{:S(2)}) copy-start(s32[2,4]{1,0:T(2,128)} %param.11) | copy-start | bytes 100
  23.6 5.4 %collective-permute-start.1 = (f32[9,4,64,12]{2,1,3,0:T(4,128)S(1)}, f32[9,4,64,12]{2,1,3,0:T(4,128)S(1)}, u32[]{:S(2)}, u32[]{:S(2)}) collective-permute-start(f32[9,4,64,12]{2,1,3,0:T(4,128)S(1)} %copy.82), channel_id=1, source_target_pairs={{4,0},{8,4},{12,8},{5,1},{9,5},{13,9},{6,2},{10,6},{14,10},{7,3},{... | collective-permute-start | bytes 331784 | tf_op jit(solution)/shard_map/ppermute | solution.py:26
  25.0 4.1 collective-permute-start
  29.0 67.1 %copy-start.16 = (f32[4,64,88,1]{2,0,1,3:T(4,128)}, f32[4,64,88,1]{2,0,1,3:T(4,128)S(1)}, u32[]{:S(2)}) copy-start(f32[4,64,88,1]{2,0,1,3:T(4,128)S(1)} %convolution_bitcast_fusion.2) | copy-start | bytes 270340
  36.2 11.7 %collective-permute-start.3 = (f32[9,4,12,152]{3,1,2,0:T(4,128)S(1)}, f32[9,4,12,152]{3,1,2,0:T(4,128)}, u32[]{:S(2)}, u32[]{:S(2)}) collective-permute-start(f32[9,4,12,152]{3,1,2,0:T(4,128)S(1)} %copy.86), channel_id=1, source_target_pairs={{16,0},{0,16},{17,1},{1,17},{18,2},{2,18},{19,3},{3,19},{20,4},{4,... | collective-permute-start | bytes 787976 | tf_op jit(solution)/shard_map/ppermute | solution.py:26
  42.8 14.6 %collective-permute-start.2 = (f32[9,4,12,152]{3,1,2,0:T(4,128)}, f32[9,4,12,152]{3,1,2,0:T(4,128)}, u32[]{:S(2)}, u32[]{:S(2)}) collective-permute-start(f32[9,4,12,152]{3,1,2,0:T(4,128)} %copy.85), channel_id=1, source_target_pairs={{0,16},{16,0},{1,17},{17,1},{2,18},{18,2},{3,19},{19,3},{4,20},{20... | collective-permute-start | bytes 787976 | tf_op jit(solution)/shard_map/ppermute | solution.py:23
  43.7 25.9 %copy-start.7 = (f32[4,128,152]{1,0,2:T(4,128)}, f32[4,128,152]{1,0,2:T(4,128)S(1)}, u32[]{:S(2)}) copy-start(f32[4,128,152]{1,0,2:T(4,128)S(1)} %fusion.16) | copy-start | bytes 933892
  73.3 6.6 %collective-permute-start.5 = (bf16[9,4,64,12]{2,1,3,0:T(4,128)(2,1)S(1)}, bf16[9,4,64,12]{2,1,3,0:T(4,128)(2,1)S(1)}, u32[]{:S(2)}, u32[]{:S(2)}) collective-permute-start(bf16[9,4,64,12]{2,1,3,0:T(4,128)(2,1)S(1)} %copy.92), channel_id=1, source_target_pairs={{4,0},{8,4},{12,8},{5,1},{9,5},{13,9},{6,2},{10,6},{14,10},{7,3},{... | collective-permute-start | bytes 165896 | tf_op jit(solution)/shard_map/ppermute | solution.py:26
  75.1 5.7 %collective-permute-start.4 = (bf16[9,4,64,12]{2,1,3,0:T(4,128)(2,1)S(1)}, bf16[9,4,64,12]{2,1,3,0:T(4,128)(2,1)S(1)}, u32[]{:S(2)}, u32[]{:S(2)}) collective-permute-start(bf16[9,4,64,12]{2,1,3,0:T(4,128)(2,1)S(1)} %copy.91), channel_id=1, source_target_pairs={{0,4},{4,8},{8,12},{1,5},{5,9},{9,13},{2,6},{6,10},{10,14},{3,7},{... | collective-permute-start | bytes 165896 | tf_op jit(solution)/shard_map/ppermute | solution.py:23
  81.7 8.1 %collective-permute-start.7 = (bf16[9,4,12,152]{3,2,0,1:T(8,128)(2,1)S(1)}, bf16[9,4,12,152]{3,2,0,1:T(8,128)(2,1)S(1)}, u32[]{:S(2)}, u32[]{:S(2)}) collective-permute-start(bf16[9,4,12,152]{3,2,0,1:T(8,128)(2,1)S(1)} %get-tuple-element.33), channel_id=1, source_target_pairs={{16,0},{0,16},{17,1},{1,17},{18,2},{2,18},{19,3},{3,19},{20,4},{4,... | collective-permute-start | bytes 393992 | tf_op jit(solution)/shard_map/ppermute | solution.py:26
  83.8 14.4 %copy-start.8 = (f32[4,128,152]{1,0,2:T(4,128)S(1)}, f32[4,128,152]{1,0,2:T(4,128)}, u32[]{:S(2)}) copy-start(f32[4,128,152]{1,0,2:T(4,128)} %copy-done.7) | copy-start | bytes 933892
  83.8 12.3 %collective-permute-start.6 = (bf16[9,4,12,152]{3,2,0,1:T(8,128)(2,1)S(1)}, bf16[9,4,12,152]{3,2,0,1:T(8,128)(2,1)S(1)}, u32[]{:S(2)}, u32[]{:S(2)}) collective-permute-start(bf16[9,4,12,152]{3,2,0,1:T(8,128)(2,1)S(1)} %get-tuple-element.32), channel_id=1, source_target_pairs={{0,16},{16,0},{1,17},{17,1},{2,18},{18,2},{3,19},{19,3},{4,20},{20... | collective-permute-start | bytes 393992 | tf_op jit(solution)/shard_map/ppermute | solution.py:23
  102.5 1.1 copy-start.20
  102.5 1.1 copy-start.19
  103.6 228.0 %all-reduce.8.cloned.1.call-start = ((), (), s32[]{:S(2)}) async-start(), calls=%async_computation.1 | async-start | bytes 524288 | tf_op jit(solution)/shard_map/psum | solution.py:101
  145.3 11.8 %copy-start.18 = (f32[1,1,2048]{2,1,0:T(1,128)S(1)}, f32[1,1,2048]{2,1,0:T(1,128)}, u32[]{:S(2)}) copy-start(f32[1,1,2048]{2,1,0:T(1,128)} %param.10) | copy-start | bytes 24580
  145.3 11.8 %copy-start.21 = (pred[2048]{0:T(1024)(128)(4,1)S(1)}, pred[2048]{0:T(1024)(128)(4,1)}, u32[]{:S(2)}) copy-start(pred[2048]{0:T(1024)(128)(4,1)} %and_reduce_fusion) | copy-start | bytes 6148
  145.3 23.4 %copy-start.5 = (f32[4,64,128]{1,2,0:T(8,128)S(1)}, f32[4,64,128]{1,2,0:T(8,128)}, u32[]{:S(2)}) copy-start(f32[4,64,128]{1,2,0:T(8,128)} %copy-done.4) | copy-start | bytes 393220
  169.2 4.9 %collective-permute-start.9 = (f32[9,4,64,12]{2,1,3,0:T(4,128)S(1)}, f32[9,4,64,12]{2,1,3,0:T(4,128)S(1)}, u32[]{:S(2)}, u32[]{:S(2)}) collective-permute-start(f32[9,4,64,12]{2,1,3,0:T(4,128)S(1)} %copy.103), channel_id=1, source_target_pairs={{4,0},{8,4},{12,8},{5,1},{9,5},{13,9},{6,2},{10,6},{14,10},{7,3},{... | collective-permute-start | bytes 331784 | tf_op jit(solution)/shard_map/ppermute | solution.py:26
  170.6 4.1 collective-permute-start.8
  174.1 0.7 copy-start.12
  174.8 0.7 copy-start.13
  182.9 11.5 %collective-permute-start.11 = (f32[9,4,12,152]{3,1,2,0:T(4,128)}, f32[9,4,12,152]{3,1,2,0:T(4,128)}, u32[]{:S(2)}, u32[]{:S(2)}) collective-permute-start(f32[9,4,12,152]{3,1,2,0:T(4,128)} %copy.107), channel_id=1, source_target_pairs={{16,0},{0,16},{17,1},{1,17},{18,2},{2,18},{19,3},{3,19},{20,4},{4,... | collective-permute-start | bytes 787976 | tf_op jit(solution)/shard_map/ppermute | solution.py:26
  188.0 15.9 %collective-permute-start.10 = (f32[9,4,12,152]{3,1,2,0:T(4,128)}, f32[9,4,12,152]{3,1,2,0:T(4,128)}, u32[]{:S(2)}, u32[]{:S(2)}) collective-permute-start(f32[9,4,12,152]{3,1,2,0:T(4,128)} %copy.106), channel_id=1, source_target_pairs={{0,16},{16,0},{1,17},{17,1},{2,18},{18,2},{3,19},{19,3},{4,20},{20... | collective-permute-start | bytes 787976 | tf_op jit(solution)/shard_map/ppermute | solution.py:23
  197.5 9.5 %copy-start.17 = (f32[4,64,88,1]{2,0,1,3:T(4,128)S(1)}, f32[4,64,88,1]{2,0,1,3:T(4,128)}, u32[]{:S(2)}) copy-start(f32[4,64,88,1]{2,0,1,3:T(4,128)} %copy-done.16) | copy-start | bytes 270340
  207.1 9.4 %copy-start.1 = (f32[9,4,64,128]{3,2,0,1:T(8,128)S(1)}, f32[9,4,64,128]{3,2,0,1:T(8,128)}, u32[]{:S(2)}) copy-start(f32[9,4,64,128]{3,2,0,1:T(8,128)} %get-tuple-element.47) | copy-start | bytes 3538948
  207.1 9.4 %copy-start.9 = (f32[4,128,152]{1,0,2:T(4,128)S(1)}, f32[4,128,152]{1,0,2:T(4,128)}, u32[]{:S(2)}) copy-start(f32[4,128,152]{1,0,2:T(4,128)} %copy-done.7) | copy-start | bytes 933892
  216.5 46.9 %copy-start.2 = (f32[9,4,64,128]{3,2,0,1:T(8,128)S(1)}, f32[9,4,64,128]{3,2,0,1:T(8,128)}, u32[]{:S(2)}) copy-start(f32[9,4,64,128]{3,2,0,1:T(8,128)} %get-tuple-element.47) | copy-start | bytes 3538948
  266.5 4.8 %collective-permute-start.13 = (bf16[9,4,64,12]{2,1,3,0:T(4,128)(2,1)S(1)}, bf16[9,4,64,12]{2,1,3,0:T(4,128)(2,1)S(1)}, u32[]{:S(2)}, u32[]{:S(2)}) collective-permute-start(bf16[9,4,64,12]{2,1,3,0:T(4,128)(2,1)S(1)} %copy.114), channel_id=1, source_target_pairs={{4,0},{8,4},{12,8},{5,1},{9,5},{13,9},{6,2},{10,6},{14,10},{7,3},{... | collective-permute-start | bytes 165896 | tf_op jit(solution)/shard_map/ppermute | solution.py:26
  268.1 4.0 collective-permute-start.12
  272.9 9.5 %collective-permute-start.15 = (bf16[9,4,12,152]{3,2,0,1:T(8,128)(2,1)S(1)}, bf16[9,4,12,152]{3,2,0,1:T(8,128)(2,1)S(1)}, u32[]{:S(2)}, u32[]{:S(2)}) collective-permute-start(bf16[9,4,12,152]{3,2,0,1:T(8,128)(2,1)S(1)} %get-tuple-element.31), channel_id=1, source_target_pairs={{16,0},{0,16},{17,1},{1,17},{18,2},{2,18},{19,3},{3,19},{20,4},{4,... | collective-permute-start | bytes 393992 | tf_op jit(solution)/shard_map/ppermute | solution.py:26
  275.3 15.5 %copy-start.10 = (f32[4,128,152]{1,0,2:T(4,128)S(1)}, f32[4,128,152]{1,0,2:T(4,128)}, u32[]{:S(2)}) copy-start(f32[4,128,152]{1,0,2:T(4,128)} %copy-done.7) | copy-start | bytes 933892
  275.3 13.4 %collective-permute-start.14 = (bf16[9,4,12,152]{3,2,0,1:T(8,128)(2,1)S(1)}, bf16[9,4,12,152]{3,2,0,1:T(8,128)(2,1)S(1)}, u32[]{:S(2)}, u32[]{:S(2)}) collective-permute-start(bf16[9,4,12,152]{3,2,0,1:T(8,128)(2,1)S(1)} %get-tuple-element.30), channel_id=1, source_target_pairs={{0,16},{16,0},{1,17},{17,1},{2,18},{18,2},{3,19},{19,3},{4,20},{20... | collective-permute-start | bytes 393992 | tf_op jit(solution)/shard_map/ppermute | solution.py:23
  334.4 11.8 %copy-start.22 = (pred[2048]{0:T(1024)(128)(4,1)S(1)}, pred[2048]{0:T(1024)(128)(4,1)}, u32[]{:S(2)}) copy-start(pred[2048]{0:T(1024)(128)(4,1)} %and_reduce_fusion) | copy-start | bytes 6148
  334.5 23.4 %copy-start.6 = (f32[4,64,128]{1,2,0:T(8,128)S(1)}, f32[4,64,128]{1,2,0:T(8,128)}, u32[]{:S(2)}) copy-start(f32[4,64,128]{1,2,0:T(8,128)} %copy-done.4) | copy-start | bytes 393220
  358.3 4.7 %collective-permute-start.17 = (f32[9,4,64,12]{2,1,3,0:T(4,128)S(1)}, f32[9,4,64,12]{2,1,3,0:T(4,128)S(1)}, u32[]{:S(2)}, u32[]{:S(2)}) collective-permute-start(f32[9,4,64,12]{2,1,3,0:T(4,128)S(1)} %copy.125), channel_id=1, source_target_pairs={{4,0},{8,4},{12,8},{5,1},{9,5},{13,9},{6,2},{10,6},{14,10},{7,3},{... | collective-permute-start | bytes 331784 | tf_op jit(solution)/shard_map/ppermute | solution.py:26
  359.7 4.1 collective-permute-start.16
  363.1 0.8 copy-start.14
  363.9 0.7 copy-start.15
  372.0 5.7 %copy-start = (f32[9,4,64,128]{3,2,0,1:T(8,128)S(1)}, f32[9,4,64,128]{3,2,0,1:T(8,128)}, u32[]{:S(2)}) copy-start(f32[9,4,64,128]{3,2,0,1:T(8,128)} %get-tuple-element.17) | copy-start | bytes 3538948
  372.0 11.5 %collective-permute-start.19 = (f32[9,4,12,152]{3,1,2,0:T(4,128)}, f32[9,4,12,152]{3,1,2,0:T(4,128)}, u32[]{:S(2)}, u32[]{:S(2)}) collective-permute-start(f32[9,4,12,152]{3,1,2,0:T(4,128)} %copy.129), channel_id=1, source_target_pairs={{16,0},{0,16},{17,1},{1,17},{18,2},{2,18},{19,3},{3,19},{20,4},{4,... | collective-permute-start | bytes 787976 | tf_op jit(solution)/shard_map/ppermute | solution.py:26
  377.1 15.8 %collective-permute-start.18 = (f32[9,4,12,152]{3,1,2,0:T(4,128)}, f32[9,4,12,152]{3,1,2,0:T(4,128)}, u32[]{:S(2)}, u32[]{:S(2)}) collective-permute-start(f32[9,4,12,152]{3,1,2,0:T(4,128)} %copy.128), channel_id=1, source_target_pairs={{0,16},{16,0},{1,17},{17,1},{2,18},{18,2},{3,19},{19,3},{4,20},{20... | collective-permute-start | bytes 787976 | tf_op jit(solution)/shard_map/ppermute | solution.py:23
  396.1 9.4 %copy-start.11 = (f32[4,128,152]{1,0,2:T(4,128)S(1)}, f32[4,128,152]{1,0,2:T(4,128)}, u32[]{:S(2)}) copy-start(f32[4,128,152]{1,0,2:T(4,128)} %copy-done.7) | copy-start | bytes 933892
  405.5 49.3 %copy-start.3 = (f32[9,4,64,128]{3,2,0,1:T(8,128)S(1)}, f32[9,4,64,128]{3,2,0,1:T(8,128)}, u32[]{:S(2)}) copy-start(f32[9,4,64,128]{3,2,0,1:T(8,128)} %get-tuple-element.47) | copy-start | bytes 3538948
Sparse Core Ops, SparseCore 0:
  103.7 38.7 all-reduce.5
  296.3 35.2 all-reduce.7
where the time goes:
time: 468 us; the launch traced here: 464 us
  waiting for transfers between devices  136 us (29%)
  local copies, waits for them, and re-layouts  86.5 us (18%)
  blocking collectives  83.3 us (18%)
  other arithmetic  50.6 us (11%)
  matrix products  50.2 us (11%)
  starting transfers between devices  36.3 us (8%)
  between operations  21.3 us (5%)
    psum x2, blocking collectives, two_products(): lax.psum((local_dot(residual, residual), local_dot(residual, hess_image))...  83.3 us
    psum x2, waiting for transfers between devices, forward(): combined = lax.psum(member_part, 'mem') + static_part  73.6 us
    ppermute x10, waiting for transfers between devices, with_halo(): lax.ppermute(lax.slice_in_dim(block, block.shape[dim] - width, None, axis...  34.1 us
    dot_general x5, matrix products, smooth(): jnp.einsum('flja,lij->flia', extended, lon_matrix, precision=lax.Precisio...  31.9 us
    ppermute x10, waiting for transfers between devices, with_halo(): lax.ppermute(lax.slice_in_dim(block, 0, width, axis=dim), axis, backward)  27.9 us
    gather x2, local copies, waits for them, and re-layouts, observe(): obs_term = jnp.where(inside, weights * flat_field[clipped], 0.0)  23.6 us
    scatter-add x2, other arithmetic, observe(): jnp.zeros((cell_count,), jnp.float32).at[clipped].add(obs_term)  22.9 us
    slice x13, local copies, waits for them, and re-layouts, with_halo(): lax.slice_in_dim(block, block.shape[dim] - width, None, axis=dim)  22.4 us
  transfers between devices with their start and end apart: 22, of which 17 were waited for; matrix products, arithmetic and copies ran while one was open for 5% of the time, Pallas kernels for 0%

commit v1 on v0

v1 whole, which is shorter than its diff:
```python
import functools
import math

import jax
import jax.numpy as jnp
from jax import lax
from jax.experimental import pallas as pl
from jax.experimental.pallas import tpu as pltpu
from jax.sharding import PartitionSpec as P

BAND = 12
RIM = 2 * BAND

hybrid_ens = 0.75
hybrid_static = 0.25

MESH = pl.DeviceIdType.MESH
VMEM = pl.BlockSpec(memory_space=pltpu.VMEM)
F32 = jnp.float32
BF16 = jnp.bfloat16


def split2(x):
    hi = x.astype(BF16)
    return hi, (x - hi.astype(F32)).astype(BF16)


def dot3(left, right):
    lh, ll = left
    rh, rl = right
    d = functools.partial(jnp.dot, preferred_element_type=F32)
    return d(lh, rh) + (d(ll, rh) + d(lh, rl))


def exchange(axis, to_low, to_high, cid):
    count = len(to_low)
    n = lax.axis_size(axis)

    def kernel(*refs):
        low_in, high_in = refs[:count], refs[count : 2 * count]
        from_low, from_high = refs[2 * count : 3 * count], refs[3 * count : 4 * count]
        send, recv = refs[4 * count :]
        me = lax.axis_index(axis)
        low, high = lax.rem(me + n - 1, n), lax.rem(me + 1, n)
        barrier = pltpu.get_barrier_semaphore()
        for other in (low, high):
            pl.semaphore_signal(barrier, inc=1, device_id={axis: other}, device_id_type=MESH)
        pl.semaphore_wait(barrier, 2)
        copies = []
        for i in range(count):
            for side, (src, dst, other) in enumerate(
                ((low_in[i], from_high[i], low), (high_in[i], from_low[i], high))
            ):
                copy = pltpu.make_async_remote_copy(
                    src_ref=src,
                    dst_ref=dst,
                    send_sem=send.at[2 * i + side],
                    recv_sem=recv.at[2 * i + side],
                    device_id={axis: other},
                    device_id_type=MESH,
                )
                copy.start()
                copies.append(copy)
        for copy in copies:
            copy.wait()

    shapes = [jax.ShapeDtypeStruct(a.shape, a.dtype) for a in (*to_high, *to_low)]
    out = pl.pallas_call(
        kernel,
        out_shape=shapes,
        in_specs=[VMEM] * (2 * count),
        out_specs=[VMEM] * (2 * count),
        scratch_shapes=[
            pltpu.SemaphoreType.DMA((2 * count,)),
            pltpu.SemaphoreType.DMA((2 * count,)),
        ],
        compiler_params=pltpu.CompilerParams(collective_id=cid, has_side_effects=True),
    )(*to_low, *to_high)
    return out[:count], out[count:]


def mem_sum(part, cid, gather):
    axis = "mem"
    n = lax.axis_size(axis)
    rows, lanes = part.shape
    chunk = rows // n

    def kernel(x_ref, out_ref, slots, send, recv, send2, recv2):
        me = lax.axis_index(axis)
        barrier = pltpu.get_barrier_semaphore()
        for j in range(1, n):
            pl.semaphore_signal(
                barrier, inc=1, device_id={axis: lax.rem(me + j, n)}, device_id_type=MESH
            )
        pl.semaphore_wait(barrier, n - 1)

        def piece(owner):
            return pl.ds(pl.multiple_of(owner * chunk, chunk), chunk)

        copies = []
        for j in range(1, n):
            peer = lax.rem(me + j, n)
            copy = pltpu.make_async_remote_copy(
                src_ref=x_ref.at[piece(peer)],
                dst_ref=slots.at[j],
                send_sem=send.at[j],
                recv_sem=recv.at[j],
                device_id={axis: peer},
                device_id_type=MESH,
            )
            copy.start()
            copies.append(copy)
        total = x_ref[piece(me), :]
        for j, copy in enumerate(copies):
            copy.wait_recv()
            total = total + slots[j + 1]
        if gather:
            out_ref[piece(me), :] = total
            back = []
            for j in range(1, n):
                peer = lax.rem(me + j, n)
                copy = pltpu.make_async_remote_copy(
                    src_ref=out_ref.at[piece(me)],
                    dst_ref=out_ref.at[piece(me)],
                    send_sem=send2.at[j],
                    recv_sem=recv2.at[j],
                    device_id={axis: peer},
                    device_id_type=MESH,
                )
                copy.start()
                back.append(copy)
            for copy in back:
                copy.wait()
        else:
            out_ref[...] = total
        for copy in copies:
            copy.wait_send()

    return pl.pallas_call(
        kernel,
        out_shape=jax.ShapeDtypeStruct((rows if gather else chunk, lanes), F32),
        in_specs=[VMEM],
        out_specs=VMEM,
        scratch_shapes=[pltpu.VMEM((n, chunk, lanes), F32)]
        + [pltpu.SemaphoreType.DMA((n,)) for _ in range(4)],
        compiler_params=pltpu.CompilerParams(collective_id=cid, has_side_effects=True),
    )(part)


def all_sum(block, cid):
    axes = ("lon", "lat", "mem")
    sizes = [lax.axis_size(a) for a in axes]
    total = math.prod(sizes)

    def kernel(x_ref, out_ref, slots, send, recv):
        mine = [lax.axis_index(a) for a in axes]

        def shifted(step):
            parts, rest = [], step
            for size in reversed(sizes):
                parts.append(rest % size)
                rest //= size
            return tuple(
                lax.rem(m + s, size) for m, s, size in zip(mine, reversed(parts), sizes)
            )

        barrier = pltpu.get_barrier_semaphore()
        for step in range(1, total):
            pl.semaphore_signal(barrier, inc=1, device_id=shifted(step), device_id_type=MESH)
        pl.semaphore_wait(barrier, total - 1)
        copies = []
        for step in range(1, total):
            copy = pltpu.make_async_remote_copy(
                src_ref=x_ref,
                dst_ref=slots.at[step],
                send_sem=send.at[step],
                recv_sem=recv.at[step],
                device_id=shifted(step),
                device_id_type=MESH,
            )
            copy.start()
            copies.append(copy)
        slots[0] = x_ref[...]
        for copy in copies:
            copy.wait()
        out_ref[...] = jnp.sum(slots[...], axis=0)

    return pl.pallas_call(
        kernel,
        out_shape=jax.ShapeDtypeStruct(block.shape, F32),
        in_specs=[VMEM],
        out_specs=VMEM,
        scratch_shapes=[
            pltpu.VMEM((total, *block.shape), F32),
            pltpu.SemaphoreType.DMA((total,)),
            pltpu.SemaphoreType.DMA((total,)),
        ],
        compiler_params=pltpu.CompilerParams(collective_id=cid, has_side_effects=True),
    )(block)


def scatter_obs(index, weight, innovation, rows, lanes):
    def kernel(i_ref, w_ref, v_ref, d_ref, b_ref):
        idx = i_ref[...]
        w = w_ref[...]
        n = idx.shape[1]
        row, lane = idx // lanes, idx % lanes
        at_row = (lax.broadcasted_iota(jnp.int32, (rows, n), 0) == row).astype(F32).astype(BF16)
        at_lane = lax.broadcasted_iota(jnp.int32, (lanes, n), 0) == lane
        for val, out in ((w, d_ref), (w * v_ref[...], b_ref)):
            acc = None
            for _ in range(3):
                part = val.astype(BF16).astype(F32)
                val = val - part
                spread_out = jnp.where(at_lane, part, 0.0).astype(BF16)
                term = lax.dot_general(
                    at_row, spread_out, (((1,), (1,)), ((), ())), preferred_element_type=F32
                )
                acc = term if acc is None else acc + term
            out[...] = acc

    return pl.pallas_call(
        kernel,
        out_shape=[jax.ShapeDtypeStruct((rows, lanes), F32)] * 2,
        in_specs=[VMEM] * 3,
        out_specs=[VMEM] * 2,
    )(index, weight, innovation)


def smooth_level(fc, fr, yc, yr, mc, mr, ml):
    fields = fc.shape[0]
    ext, lanes = yc.shape
    xc = (fc[...] * yc[None]).reshape(fields * ext, lanes)
    xr = (fr[...] * yr[None]).reshape(fields * ext, yr.shape[1])
    t = dot3(split2(xc), split2(mc)) + dot3(split2(xr), split2(mr))
    th, tl = split2(t)
    lon = split2(ml)
    return [
        dot3(lon, (th[f * ext : (f + 1) * ext], tl[f * ext : (f + 1) * ext]))
        for f in range(fields)
    ]


def apply_cov(fc, fr, yc, yr, mats, lon_cells, mem_count):
    levels, fields, ext, lanes = fc.shape
    mc, mr, ml = mats

    def kernel(fc_ref, fr_ref, yc_ref, yr_ref, mc_ref, mr_ref, ml_ref, out_ref):
        smoothed = smooth_level(
            fc_ref.at[0], fr_ref, yc_ref[0], yr_ref[...], mc_ref[0], mr_ref[0], ml_ref[0]
        )
        acc = fc_ref[0, fields - 1, :lon_cells, :] * smoothed[-1] * (1.0 / mem_count)
        for f in range(fields - 1):
            acc = acc + fc_ref[0, f, :lon_cells, :] * smoothed[f]
        out_ref[0] = acc

    def level(*shape):
        return pl.BlockSpec((1, *shape), lambda l: (l,) + (0,) * len(shape))

    return pl.pallas_call(
        kernel,
        grid=(levels,),
        out_shape=jax.ShapeDtypeStruct((levels, lon_cells, lanes), F32),
        in_specs=[
            level(*fc.shape[1:]),
            VMEM,
            level(*yc.shape[1:]),
            VMEM,
            level(*mc.shape[1:]),
            level(*mr.shape[1:]),
            level(*ml.shape[1:]),
        ],
        out_specs=level(lon_cells, lanes),
    )(fc, fr, yc, yr, mc, mr, ml)


def apply_adjoint(fc, fr, yc, yr, mats, lon_cells):
    levels, fields, ext, lanes = fc.shape
    mc, mr, ml = mats

    def kernel(fc_ref, fr_ref, yc_ref, yr_ref, mc_ref, mr_ref, ml_ref, ens_ref, static_ref):
        smoothed = smooth_level(
            fc_ref.at[0], fr_ref, yc_ref[0], yr_ref[...], mc_ref[0], mr_ref[0], ml_ref[0]
        )
        for f in range(fields - 1):
            ens_ref[f, 0] = smoothed[f]
        static_ref[0] = smoothed[-1]

    def level(*shape):
        return pl.BlockSpec((1, *shape), lambda l: (l,) + (0,) * len(shape))

    return pl.pallas_call(
        kernel,
        grid=(levels,),
        out_shape=[
            jax.ShapeDtypeStruct((fields - 1, levels, lon_cells, lanes), F32),
            jax.ShapeDtypeStruct((levels, lon_cells, lanes), F32),
        ],
        in_specs=[
            level(*fc.shape[1:]),
            VMEM,
            level(*yc.shape[1:]),
            VMEM,
            level(*mc.shape[1:]),
            level(*mr.shape[1:]),
            level(*ml.shape[1:]),
        ],
        out_specs=[
            pl.BlockSpec((fields - 1, 1, lon_cells, lanes), lambda l: (0, l, 0, 0)),
            level(lon_cells, lanes),
        ],
    )(fc, fr, yc, yr, mc, mr, ml)


def pack_lat(x, side):
    lanes = x.shape[-1]
    cut = slice(0, RIM) if side == 0 else slice(lanes - RIM, lanes)
    return jnp.concatenate([x[..., l, :, cut] for l in range(x.shape[-3])], axis=-1)


def rows_of(x, side):
    rows = x.shape[-2]
    return x[..., :RIM, :] if side == 0 else x[..., rows - RIM :, :]


def extend(arrays, cids):
    lat_n = lax.axis_size("lat")
    at = lax.axis_index("lat")
    lows, highs = exchange(
        "lat", [pack_lat(x, 0) for x in arrays], [pack_lat(x, 1) for x in arrays], cids[0]
    )
    rims = []
    for low, high in zip(lows, highs):
        low = jnp.where(at > 0, low, jnp.zeros_like(low))
        high = jnp.where(at < lat_n - 1, high, jnp.zeros_like(high))
        rims.append((low, high))

    def lon_pack(x, rim, side):
        body = rows_of(x, side)
        body = body.reshape(*x.shape[:-3], x.shape[-3] * RIM, x.shape[-1])
        edge = jnp.concatenate([rows_of(rim[0], side), rows_of(rim[1], side)], axis=-2)
        return body, edge

    to_low, to_high = [], []
    for x, rim in zip(arrays, rims):
        to_low.extend(lon_pack(x, rim, 0))
        to_high.extend(lon_pack(x, rim, 1))
    from_low, from_high = exchange("lon", to_low, to_high, cids[1])
    out = []
    for i, (x, rim) in enumerate(zip(arrays, rims)):
        shape = (*x.shape[:-2], RIM, x.shape[-1])
        center = jnp.concatenate(
            [x, from_low[2 * i].reshape(shape), from_high[2 * i].reshape(shape)], axis=-2
        )
        sides = []
        for s in range(2):
            cut = slice(s * RIM, (s + 1) * RIM)
            sides.append(
                jnp.concatenate(
                    [rim[s], from_low[2 * i + 1][..., cut, :], from_high[2 * i + 1][..., cut, :]],
                    axis=-2,
                )
            )
        out.append((center, jnp.concatenate(sides, axis=-1)))
    return out


def band_weight(widths, offset):
    w = widths.astype(F32)
    taps = jnp.arange(-BAND, BAND + 1).astype(F32)

    def shape_of(o, width):
        raw = jnp.exp(-0.5 * (o / (0.5 * width)) ** 2)
        return jnp.where(jnp.abs(o) <= width, raw, 0.0)

    norm = jnp.sum(shape_of(taps[None, :], w[:, None]), axis=1)
    return shape_of(offset.astype(F32)[None], w[:, None, None]) / norm[:, None, None]


def matrices(band_width, lon_cells, lat_cells):
    levels = band_width.shape[1]
    mm = functools.partial(jnp.einsum, precision=lax.Precision.HIGHEST)
    own = jnp.arange(lon_cells)
    ext = jnp.concatenate([own, jnp.arange(-RIM, 0), lon_cells + jnp.arange(RIM)])
    mid = jnp.arange(-BAND, lon_cells + BAND)
    first = band_weight(band_width[0], own[:, None] - mid[None, :])
    second = band_weight(band_width[0], mid[:, None] - ext[None, :])
    lon_two = mm("lim,lmj->lij", first, second)
    lon_one = band_weight(band_width[0], own[:, None] - ext[None, :])
    own = jnp.arange(lat_cells)
    ext = jnp.concatenate([own, jnp.arange(-RIM, 0), lat_cells + jnp.arange(RIM)])
    mid = jnp.arange(-BAND, lat_cells + BAND)
    place = lax.axis_index("lat") * lat_cells + mid
    inside = (place >= 0) & (place < lat_cells * lax.axis_size("lat"))
    first = band_weight(band_width[1], ext[:, None] - mid[None, :])
    second = band_weight(band_width[1], mid[:, None] - own[None, :])
    second = jnp.where(inside[None, :, None], second, 0.0)
    lat_two = mm("lim,lmj->lij", first, second)
    lat_one = band_weight(band_width[1], ext[:, None] - own[None, :])

    def halves(lat):
        sel = jnp.eye(levels, dtype=F32)
        rims = []
        for s in range(2):
            part = lat[:, lat_cells + s * RIM : lat_cells + (s + 1) * RIM]
            rims.append(
                (sel[:, :, None, None] * part[:, None]).reshape(levels, levels * RIM, lat_cells)
            )
        return lat[:, :lat_cells], jnp.concatenate(rims, axis=1)

    return (*halves(lat_two), lon_two), (*halves(lat_one), lon_one)


def per_device(anomalies, spread, obs_index, innovation, obs_weight, band_width):
    members = anomalies.shape[0]
    levels, lon_cells, lat_cells = spread.shape
    mem_count = lax.axis_size("mem")
    coef_ens = math.sqrt(hybrid_ens / (members * mem_count))
    coef_static = math.sqrt(hybrid_static)
    rows = levels * lon_cells
    field = (levels, lon_cells, lat_cells)

    diag, rhs = scatter_obs(
        obs_index.reshape(1, -1), obs_weight.reshape(1, -1), innovation.reshape(1, -1), rows, lat_cells
    )
    two, one = matrices(band_width, lon_cells, lat_cells)

    (ac, ar), (sc, sr), (bc, br) = extend([anomalies, spread, rhs.reshape(field)], (0, 1))
    ac = jnp.swapaxes(ac, 0, 1).astype(F32)
    fc = jnp.concatenate([coef_ens * ac, coef_static * sc[:, None]], axis=1)
    fr = jnp.concatenate([coef_ens * ar.astype(F32), coef_static * sr[None]], axis=0)

    cov_b = mem_sum(
        apply_cov(fc, fr, bc, br, two, lon_cells, mem_count).reshape(rows, lat_cells), 2, True
    )
    image = rhs + diag * cov_b
    scale = 1.0 / mem_count

    def dots(left, right):
        a = jnp.sum(left.reshape(-1, 8, lat_cells), axis=0)
        b = jnp.sum(right.reshape(-1, 8, lat_cells), axis=0)
        a, b = jnp.sum(a, axis=0, keepdims=True), jnp.sum(b, axis=0, keepdims=True)
        pad = jnp.zeros((6, lat_cells), F32)
        total = jnp.sum(all_sum(jnp.concatenate([a, b, pad], axis=0), 3), axis=1)
        return total[0], total[1]

    norm0, curve0 = dots(scale * (rhs * cov_b), scale * (cov_b * image))
    alpha0 = norm0 / curve0
    ((qc, qr),) = extend([image.reshape(field)], (4, 5))
    cov_q = mem_sum(
        apply_cov(fc, fr, qc, qr, two, lon_cells, mem_count).reshape(rows, lat_cells), 6, False
    )
    chunk = rows // mem_count
    start = lax.axis_index("mem") * chunk

    def mine(x):
        return lax.dynamic_slice_in_dim(x, start, chunk, axis=0)

    resid = mine(rhs) - alpha0 * mine(image)
    cov_r = mine(cov_b) - alpha0 * cov_q
    norm1, curve1 = dots(resid * cov_r, cov_r * (resid + mine(diag) * cov_r))
    beta = norm1 / norm0
    alpha1 = norm1 / (curve1 - beta * norm1 / alpha0)
    cc = alpha0 * bc + alpha1 * ((bc - alpha0 * qc) + beta * bc)
    cr = alpha0 * br + alpha1 * ((br - alpha0 * qr) + beta * br)
    ens, static = apply_adjoint(fc, fr, cc, cr, one, lon_cells)
    return ens, static


def solution(mesh):
    return jax.shard_map(
        per_device,
        mesh=mesh,
        in_specs=(
            P("mem", None, "lon", "lat"),
            P(None, "lon", "lat"),
            P("lon", "lat", None),
            P("lon", "lat", None),
            P("lon", "lat", None),
            P(),
        ),
        out_specs=(P("mem", None, "lon", "lat"), P(None, "lon", "lat")),
        check_vma=False,
    )
```

time: 468 us -> 169 us (0.36)
  waiting for transfers between devices: 136 us -> 0 us
  Pallas kernels: 0 us -> 117 us
  blocking collectives: 83.3 us -> 0 us
  local copies, waits for them, and re-layouts: 86.5 us -> 10.9 us
  matrix products: 50.2 us -> 2.9 us
  starting transfers between devices: 36.3 us -> 0 us
  other arithmetic: 50.6 us -> 30.1 us
  between operations: 21.3 us -> 7.1 us
    pallas_call x0 -> x12, Pallas kernels: none -> 117 us  [the longest x4 46.6 us: exchange(): pl.pallas_call(kernel, out_shape=shapes, in_specs=[VMEM] * (2 * count), o...]
    psum x2 -> x0, blocking collectives: 83.3 us -> none  [two_products(): lax.psum((local_dot(residual, residual), local_dot(residual, hess_image))...]
    psum x2 -> x0, waiting for transfers between devices: 73.6 us -> none  [forward(): combined = lax.psum(member_part, 'mem') + static_part]
    ppermute x20 -> x0, waiting for transfers between devices: 62.1 us -> none  [the longest x10 34.1 us: with_halo(): lax.ppermute(lax.slice_in_dim(block, block.shape[dim] - width, None, axis...]
    dot_general x12 -> x2, matrix products: 50.2 us -> 2.9 us  [the longest x1 1.8 us: matrices(): lat_two = mm('lim,lmj->lij', first, second)]
    ppermute x20 -> x0, starting transfers between devices: 36.3 us -> none  [the longest x10 19.2 us: with_halo(): lax.ppermute(lax.slice_in_dim(block, block.shape[dim] - width, None, axis...]
    scatter-add x3 -> x0, other arithmetic: 34.1 us -> none  [the longest x2 22.9 us: observe(): jnp.zeros((cell_count,), jnp.float32).at[clipped].add(obs_term)]
    slice x22 -> x26, local copies, waits for them, and re-layouts: 33.8 us -> 7.89 us  [the longest x12 3.79 us: rows_of(): return x[..., :RIM, :] if side == 0 else x[..., rows - RIM:, :]]
  transfers between devices with their start and end apart: 22 -> 0, of which waited for: 17 -> 0; matrix products, arithmetic and copies ran while one was open for 5% -> 0% of each run, Pallas kernels for 0% -> 0%
where the time goes in v1:
time: 169 us; the launch traced here: 168 us
  Pallas kernels  117 us (69%)
  other arithmetic  30.1 us (18%)
  local copies, waits for them, and re-layouts  10.9 us (6%)
  between operations  7.1 us (4%)
  matrix products  2.9 us (2%)
    pallas_call x4, Pallas kernels, exchange(): pl.pallas_call(kernel, out_shape=shapes, in_specs=[VMEM] * (2 * count), o...  46.6 us
    pallas_call x2, Pallas kernels, mem_sum(): pl.pallas_call(kernel, out_shape=jax.ShapeDtypeStruct((rows if gather els...  21.9 us
    pallas_call x2, Pallas kernels, all_sum(): pl.pallas_call(kernel, out_shape=jax.ShapeDtypeStruct(block.shape, F32),...  21.2 us
    pallas_call x2, Pallas kernels, apply_cov(): pl.pallas_call(kernel, grid=(levels,), out_shape=jax.ShapeDtypeStruct((le...  16.2 us
    pallas_call x1, Pallas kernels, apply_adjoint(): pl.pallas_call(kernel, grid=(levels,), out_shape=[jax.ShapeDtypeStruct((f...  8.01 us
    concatenate x8, other arithmetic, lon_pack(): jnp.concatenate([rows_of(rim[0], side), rows_of(rim[1], side)], axis=-2)  4.94 us
    concatenate x5, other arithmetic, pack_lat(): jnp.concatenate([x[..., l, :, cut] for l in range(x.shape[-3])], axis=-1)  3.97 us
    slice x12, local copies, waits for them, and re-layouts, rows_of(): return x[..., :RIM, :] if side == 0 else x[..., rows - RIM:, :]  3.79 us

profile of v1, /device:TPU:0, one launch (start us, length us, event | category | flops | bytes accessed | tf_op | source)
XLA Modules:
  0.0 168.1 jit_solution(18387511541903500832)
XLA Ops:
  0.6 1.8 %fusion.84 = (bf16[8,4,24,128]{3,2,1,0:T(8,128)(2,1)}, bf16[8,4,24,128]{3,2,1,0:T(8,128)(2,1)}) fusion(bf16[8,4,64,128]{3,2,1,0:T(8,128)(2,1)} %param.6), kind=kLoop, calls=%fused_computation.194 | loop fusion | bytes 786432 | tf_op jit(solution)/shard_map/slice | solution.py:323
  2.4 1.6 slice_bitcast_fusion.3
  4.0 1.1 pad_maximum_fusion.7
  5.2 0.8 pad_maximum_fusion.11
  5.9 3.2 %shard_map.77 = (f32[256,128]{1,0:T(8,128)}, f32[256,128]{1,0:T(8,128)}) custom-call(s32[1,2048]{1,0:T(1,128)} %bitcast.165, f32[1,2048]{1,0:T(1,128)} %bitcast.166, f32[1,2048]{1,0:T(1,128)} %bitcast.167), custom_call_target="tpu_custom_call" | custom-call | tf_op jit(solution)/shard_map/pallas_call | solution.py:222
  9.2 1.0 slice_bitcast_fusion.19
  10.2 0.8 pad_maximum_fusion.12
  10.9 10.3 %shard_map.78 = (bf16[8,64,96]{2,1,0:T(8,128)(2,1)}, f32[64,96]{1,0:T(8,128)}, f32[64,96]{1,0:T(8,128)}, bf16[8,64,96]{2,1,0:T(8,128)(2,1)}, f32[64,96]{1,0:T(8,128)}, /*index=5*/f32[64,96]{1,0:T(8,128)}) custom-call(bf16[8,64,96]{2,1,0:T(8,128)(2,1)} %get-tuple-element.149.refs_0_, f32[64,96]{1,0:T(8,128)} %get-tuple-element.151.refs_1_, ...), custom_call_target="tpu_custom_call" | custom-call | tf_op jit(solution)/shard_map/pallas_call | solution.py:68
  21.2 1.0 broadcast_select_fusion
  22.3 0.7 pad_maximum_fusion.9.refs_1_
  23.0 0.6 fusion.89
  23.6 0.8 broadcast_select_fusion.6
  24.4 0.6 pad_maximum_fusion.17.refs_3_
  25.0 0.7 fusion.88
  25.7 0.6 pad_maximum_fusion.18.refs_5_
  26.3 0.7 pad_maximum_fusion.10.refs_7_
  27.0 0.6 pad_maximum_fusion.19.refs_9_
  27.6 0.6 pad_maximum_fusion.20.refs_11_
  28.2 24.1 %shard_map.79 = (bf16[8,96,128]{2,1,0:T(8,128)(2,1)}, bf16[8,48,96]{2,1,0:T(8,128)(2,1)}, f32[96,128]{1,0:T(8,128)}, f32[48,96]{1,0:T(8,128)}, f32[96,128]{1,0:T...) custom-call(bf16[8,96,128]{2,1,0:T(8,128)(2,1)} %bitcast.144, ...), custom_call_target="tpu_custom_call" | custom-call | tf_op jit(solution)/shard_map/pallas_call | solution.py:68
  52.3 0.8 maximum_multiply_fusion
  53.2 1.2 multiply_bitcast_fusion
  54.4 1.5 pad_maximum_fusion.fc_ref
  56.2 0.2 convert_multiply_fusion
  56.4 1.1 pad_maximum_fusion.1.fr_ref
  57.4 0.7 pad_maximum_fusion.5.yc_ref
  58.2 0.7 maximum_maximum_fusion.yr_ref
  59.0 0.2 fusion.76
  59.7 1.8 %fusion.4 = f32[4,176,128]{2,1,0:T(8,128)S(1)} fusion(f32[4]{0:T(128)S(1)} %get-tuple-element.59, f32[4]{0:T(128)S(1)} %get-tuple-element.143, f32[176,152]{0,1:T(8,128)S(1)} %subtract_convert_fusion, f32[176,152]{0,1:T(8,128)S(1)} %fusion.64, f32[4]{0:T(128)S(1)} %get-tuple-element.141, f32[152,128]{1,0:T(8,128)S(1)} %subtract_convert_fusion.2, ...), kind=kOutput, calls=%fused_computation.10 | convolution fusion | flops 165551104 | bytes 730312 | tf_op jit(solution)/shard_map/lim,lmj->lij/dot_general | solution.py:398
  61.5 0.7 slice.362.mc_ref
  62.4 0.2 fusion.10
  62.9 0.8 pad_maximum_fusion.3.mr_ref
  63.9 1.1 fusion.29.ml_ref
  65.0 8.1 %shard_map.80 = f32[4,64,128]{2,1,0:T(8,128)} custom-call(f32[4,9,112,128]{3,2,1,0:T(8,128)} %pad_maximum_fusion.fc_ref, f32[9,112,192]{2,1,0:T(8,128)} %pad_maximum_fusion.1.fr_ref, f32[4,112,128]{2,1,0:T(8,128)} %pad_maximum_fusion.5.yc_ref, f32[112,192]{1,0:T(8,128)} %maximum_maximum_fusion.yr_ref, f32[4,128,128]{2,1,0:T(8,128)} %slice.362.mc_ref, ...), custom_call_target="tpu_custom_call" | custom-call | tf_op jit(solution)/shard_map/pallas_call | solution.py:260
  73.1 14.5 %shard_map.81 = f32[256,128]{1,0:T(8,128)} custom-call(f32[256,128]{1,0:T(8,128)} %bitcast.146), custom_call_target="tpu_custom_call" | custom-call | tf_op jit(solution)/shard_map/pallas_call | solution.py:139
  87.7 1.0 multiply_reduce_fusion.1
  88.6 0.6 fusion.87
  89.4 0.7 pad_maximum_fusion.15.refs_0_
  90.1 0.7 pad_maximum_fusion.16.refs_1_
  90.8 4.8 %shard_map.83 = (f32[64,96]{1,0:T(8,128)}, f32[64,96]{1,0:T(8,128)}) custom-call(f32[64,96]{1,0:T(8,128)} %pad_maximum_fusion.15.refs_0_, f32[64,96]{1,0:T(8,128)} %pad_maximum_fusion.16.refs_1_), custom_call_target="tpu_custom_call" | custom-call | tf_op jit(solution)/shard_map/pallas_call | solution.py:68
  95.5 0.8 broadcast_select_fusion.2
  96.3 0.6 pad_maximum_fusion.21.refs_1_
  96.9 0.6 pad_maximum_fusion.22.refs_3_
  97.5 7.4 %shard_map.84 = (f32[96,128]{1,0:T(8,128)}, f32[48,96]{1,0:T(8,128)}, f32[96,128]{1,0:T(8,128)}, f32[48,96]{1,0:T(8,128)}) custom-call(f32[96,128]{1,0:T(8,128)} %bitcast.160, f32[48,96]{1,0:T(8,128)} %pad_maximum_fusion.21.refs_1_, f32[96,128]{1,0:T(8,128)} %bitcast.159, f32[48,96]{1,0:T(8,128)} %pad_maximum_fusion.22.refs_3_), custom_call_target="tpu_custom_call" | custom-call | tf_op jit(solution)/shard_map/pallas_call | solution.py:68
  105.0 1.5 pad_maximum_fusion.6.yc_ref
  106.5 0.7 fusion.101
  107.3 0.7 fusion.100
  108.0 0.7 maximum_maximum_fusion.1.yr_ref
  108.7 8.1 %shard_map.85 = f32[4,64,128]{2,1,0:T(8,128)} custom-call(f32[4,9,112,128]{3,2,1,0:T(8,128)} %pad_maximum_fusion.fc_ref, f32[9,112,192]{2,1,0:T(8,128)} %pad_maximum_fusion.1.fr_ref, f32[4,112,128]{2,1,0:T(8,128)} %pad_maximum_fusion.6.yc_ref, f32[112,192]{1,0:T(8,128)} %maximum_maximum_fusion.1.yr_ref, f32[4,128,128]{2,1,0:T(8,128)} %slice.362.mc_ref, ...), custom_call_target="tpu_custom_call" | custom-call | tf_op jit(solution)/shard_map/pallas_call | solution.py:260
  116.8 7.4 %shard_map.86 = f32[64,128]{1,0:T(8,128)} custom-call(f32[256,128]{1,0:T(8,128)} %bitcast.145), custom_call_target="tpu_custom_call" | custom-call | tf_op jit(solution)/shard_map/pallas_call | solution.py:139
  124.3 0.7 maximum_maximum_fusion.2.x_ref
  124.9 10.7 %shard_map.82 = f32[8,128]{1,0:T(8,128)} custom-call(f32[8,128]{1,0:T(8,128)} %maximum_maximum_fusion.2.x_ref), custom_call_target="tpu_custom_call" | custom-call | tf_op jit(solution)/shard_map/pallas_call | solution.py:188
  135.7 0.8 reduce_sum.77
  136.5 0.6 fusion.107
  138.4 0.8 multiply_reduce_fusion.3
  139.2 0.7 maximum_maximum_fusion.3.x_ref
  139.8 10.5 %shard_map.87 = f32[8,128]{1,0:T(8,128)} custom-call(f32[8,128]{1,0:T(8,128)} %maximum_maximum_fusion.3.x_ref), custom_call_target="tpu_custom_call" | custom-call | tf_op jit(solution)/shard_map/pallas_call | solution.py:188
  150.3 0.8 reduce_sum.83
  151.1 0.6 fusion.106
  156.3 0.8 multiply_add_fusion.yc_ref
  157.0 0.8 multiply_add_fusion.2.yr_ref
  157.8 0.7 slice.379.mc_ref
  158.5 0.8 pad_maximum_fusion.4.mr_ref
  159.3 0.8 fusion.43.ml_ref
  160.1 8.0 %shard_map.88 = (f32[8,4,64,128]{3,2,1,0:T(8,128)}, f32[4,64,128]{2,1,0:T(8,128)}) custom-call(f32[4,9,112,128]{3,2,1,0:T(8,128)} %pad_maximum_fusion.fc_ref, f32[9,112,192]{2,1,0:T(8,128)} %pad_maximum_fusion.1.fr_ref, f32[4,112,128]{2,1,0:T(8,128)} %multiply_add_fusion.yc_ref, f32[112,192]{1,0:T(8,128)} %multiply_add_fusion.2.yr_ref, ...), custom_call_target="tpu_custom_call" | custom-call | tf_op jit(solution)/shard_map/pallas_call | solution.py:292
  (91 shorter events, 1.8 us)
Async XLA Ops:
  2.4 2.6 %copy-start.2 = (f32[4,64,128]{2,1,0:T(8,128)S(1)}, f32[4,64,128]{2,1,0:T(8,128)}, u32[]{:S(2)}) copy-start(f32[4,64,128]{2,1,0:T(8,128)} %param.7) | copy-start | bytes 393220
  9.2 15.8 %copy-start.1 = (f32[256,128]{1,0:T(8,128)S(1)}, f32[256,128]{1,0:T(8,128)}, u32[]{:S(2)}) copy-start(f32[256,128]{1,0:T(8,128)} %get-tuple-element.28) | copy-start | bytes 393220
  21.2 4.5 %copy-start.11 = (f32[64,96]{1,0:T(8,128)S(1)}, f32[64,96]{1,0:T(8,128)}, u32[]{:S(2)}) copy-start(f32[64,96]{1,0:T(8,128)} %get-tuple-element.34) | copy-start | bytes 73732
  21.2 4.5 %copy-start.10 = (f32[64,96]{1,0:T(8,128)S(1)}, f32[64,96]{1,0:T(8,128)}, u32[]{:S(2)}) copy-start(f32[64,96]{1,0:T(8,128)} %get-tuple-element.33) | copy-start | bytes 73732
  21.2 31.9 %copy-start = (bf16[8,4,64,128]{3,2,1,0:T(8,128)(2,1)S(1)}, bf16[8,4,64,128]{3,2,1,0:T(8,128)(2,1)}, u32[]{:S(2)}) copy-start(bf16[8,4,64,128]{3,2,1,0:T(8,128)(2,1)} %param.6) | copy-start | bytes 1572868
  54.4 1.5 copy-start.15
  54.4 1.5 copy-start.14
  54.4 1.7 copy-start.9
  54.4 1.7 %copy-start.8 = (bf16[8,48,96]{2,1,0:T(8,128)(2,1)S(1)}, bf16[8,48,96]{2,1,0:T(8,128)(2,1)}, u32[]{:S(2)}) copy-start(bf16[8,48,96]{2,1,0:T(8,128)(2,1)} %get-tuple-element.39) | copy-start | bytes 221188
  56.1 1.4 copy-start.4
  56.1 1.4 copy-start.5
  56.1 2.0 %copy-start.13 = (f32[48,96]{1,0:T(8,128)S(1)}, f32[48,96]{1,0:T(8,128)}, u32[]{:S(2)}) copy-start(f32[48,96]{1,0:T(8,128)} %get-tuple-element.46) | copy-start | bytes 55300
  56.1 2.0 %copy-start.12 = (f32[48,96]{1,0:T(8,128)S(1)}, f32[48,96]{1,0:T(8,128)}, u32[]{:S(2)}) copy-start(f32[48,96]{1,0:T(8,128)} %get-tuple-element.45) | copy-start | bytes 55300
  56.2 2.8 %copy-start.16 = (s32[2,4]{1,0:T(2,128)S(1)}, s32[2,4]{1,0:T(2,128)}, u32[]{:S(2)}) copy-start(s32[2,4]{1,0:T(2,128)} %param.11) | copy-start | bytes 100
  65.0 22.6 %copy-start.3 = (f32[256,128]{1,0:T(8,128)S(1)}, f32[256,128]{1,0:T(8,128)}, u32[]{:S(2)}) copy-start(f32[256,128]{1,0:T(8,128)} %get-tuple-element.47) | copy-start | bytes 393220
  108.7 47.5 %copy-start.6 = (f32[96,128]{1,0:T(8,128)S(1)}, f32[96,128]{1,0:T(8,128)}, u32[]{:S(2)}) copy-start(f32[96,128]{1,0:T(8,128)} %get-tuple-element.50) | copy-start | bytes 147460
  108.7 47.5 %copy-start.7 = (f32[96,128]{1,0:T(8,128)S(1)}, f32[96,128]{1,0:T(8,128)}, u32[]{:S(2)}) copy-start(f32[96,128]{1,0:T(8,128)} %get-tuple-element.51) | copy-start | bytes 147460

commit v2 on v0

v2 whole, which is shorter than its diff:
```python
import functools
import math

import jax
import jax.numpy as jnp
from jax import lax
from jax.experimental import pallas as pl
from jax.experimental.pallas import tpu as pltpu
from jax.sharding import PartitionSpec as P

BAND = 12
RIM = 2 * BAND

hybrid_ens = 0.75
hybrid_static = 0.25

MESH = pl.DeviceIdType.MESH
VMEM = pl.BlockSpec(memory_space=pltpu.VMEM)
F32 = jnp.float32
BF16 = jnp.bfloat16


def split2(x):
    hi = x.astype(BF16)
    return hi, (x - hi.astype(F32)).astype(BF16)


def dot3(left, right):
    lh, ll = left
    rh, rl = right
    d = functools.partial(jnp.dot, preferred_element_type=F32)
    return d(lh, rh) + (d(ll, rh) + d(lh, rl))


AXES = ("lon", "lat", "mem")


def fused(a_ref, s_ref, i_ref, w_ref, v_ref, bw_ref, ens_ref, static_ref, *scratch, dims):
    members, levels, lon_cells, lat_cells, sizes = dims
    (fc, fr, bc, br, qc, qr, send_al, send_ah, recv_al, recv_ah, pack_l, pack_h, recv_pl, recv_ph,
     fpack, xrh, xrl, two_c, two_r, two_l, one_c, one_r, one_l, bflat, dflat, cov, part,
     slots, slots2, dslots, dsend, send, recv, csend, crecv, dsems, drems) = scratch
    lon_n, lat_n, mem_n = sizes
    total = lon_n * lat_n * mem_n
    fields = members + 1
    ext = lon_cells + 2 * RIM
    rows = levels * lon_cells
    chunk = rows // mem_n
    coef_ens = math.sqrt(hybrid_ens / (members * mem_n))
    coef_static = math.sqrt(hybrid_static)
    mine = [lax.axis_index(a) for a in AXES]
    lat_at, me = mine[1], mine[2]
    has_low, has_high = lat_at > 0, lat_at < lat_n - 1

    def shifted(step):
        parts, rest = [], step
        for size in reversed(sizes):
            parts.append(rest % size)
            rest //= size
        return tuple(lax.rem(m + s, size) for m, s, size in zip(mine, reversed(parts), sizes))

    barrier = pltpu.get_barrier_semaphore()
    for step in range(1, total):
        pl.semaphore_signal(barrier, inc=1, device_id=shifted(step), device_id_type=MESH)

    used = [0]

    def remote(src, dst, where):
        k = used[0]
        used[0] += 1
        return pltpu.make_async_remote_copy(
            src_ref=src, dst_ref=dst, send_sem=send.at[k], recv_sem=recv.at[k],
            device_id=where, device_id_type=MESH,
        )

    lon_low = {"lon": lax.rem(mine[0] + lon_n - 1, lon_n)}
    lon_high = {"lon": lax.rem(mine[0] + 1, lon_n)}
    lat_low = {"lat": lax.rem(lat_at + lat_n - 1, lat_n)}
    lat_high = {"lat": lax.rem(lat_at + 1, lat_n)}
    own = pl.ds(0, lon_cells)
    rim = pl.ds(lon_cells, 2 * RIM)
    low_rows = pl.ds(lon_cells, RIM)
    high_rows = pl.ds(lon_cells + RIM, RIM)
    first_rows = pl.ds(0, RIM)
    last_rows = pl.ds(lon_cells - RIM, RIM)
    low_lanes = pl.ds(0, lat_cells)
    high_lanes = pl.ds(lat_cells, lat_cells)

    def lon_start(copies):
        for c in copies:
            c.start()

    def lon_wait(copies):
        for c in copies:
            c.wait()

    class Lat:
        def __init__(self, low_src, high_src, from_low, from_high):
            self.to_low = remote(low_src, from_high, lat_low)
            self.to_high = remote(high_src, from_low, lat_high)

        def start(self):
            pl.when(has_low)(self.to_low.start)
            pl.when(has_high)(self.to_high.start)

        def wait(self):
            pl.when(has_low)(self.to_low.wait_send)
            pl.when(has_high)(self.to_high.wait_send)
            pl.when(has_high)(self.to_low.wait_recv)
            pl.when(has_low)(self.to_high.wait_recv)

    def lane_pack(read, count):
        lane = lax.broadcasted_iota(jnp.int32, (count, lat_cells), 1)
        low = jnp.zeros((count, lat_cells), F32)
        high = low
        for l in range(levels):
            x = read(l)
            here = (lane >= l * RIM) & (lane < (l + 1) * RIM)
            low = jnp.where(here, pltpu.roll(x, (l * RIM) % lat_cells, 1), low)
            high = jnp.where(here, pltpu.roll(x, ((l + 1) * RIM) % lat_cells, 1), high)
        return low, high

    def zero_edges(ref, lead=()):
        @pl.when(jnp.logical_not(has_low))
        def _():
            ref[(*lead, slice(None), low_lanes)] = jnp.zeros((ext, lat_cells), F32)

        @pl.when(jnp.logical_not(has_high))
        def _():
            ref[(*lead, slice(None), high_lanes)] = jnp.zeros((ext, lat_cells), F32)

    def load_member(m, _):
        lows, highs = [], []
        for l in range(levels):
            x = a_ref[m, l].astype(F32)
            fc[l, m, :lon_cells, :] = x
            lows.append(x[:RIM])
            highs.append(x[lon_cells - RIM :])
        send_al[m] = jnp.concatenate(lows, axis=0).astype(BF16)
        send_ah[m] = jnp.concatenate(highs, axis=0).astype(BF16)
        return 0

    lax.fori_loop(0, members, load_member, 0)
    for l in range(levels):
        fc[l, members, :lon_cells, :] = s_ref[l]

    def pack_member(span, count):
        def go(m, _):
            low, high = lane_pack(lambda l: fc[l, m, span, :], count)
            pack_l[m, span, :] = low.astype(BF16)
            pack_h[m, span, :] = high.astype(BF16)
            return 0

        lax.fori_loop(0, members, go, 0)

    def lon_field(ref, lead):
        at = lambda span: ref.at[(slice(None), *lead, span, slice(None))]
        return [
            remote(at(first_rows), at(high_rows), lon_low),
            remote(at(last_rows), at(low_rows), lon_high),
        ]

    def lat_field(slot, dst, lead, span):
        at = lambda lanes: dst.at[(*lead, span, lanes)]
        return Lat(
            fpack.at[slot, 0, span, :], fpack.at[slot, 1, span, :], at(low_lanes), at(high_lanes)
        )

    def fill_pack(slot, read, span, count):
        low, high = lane_pack(lambda l: read(l, span), count)
        fpack[slot, 0, span, :] = low
        fpack[slot, 1, span, :] = high

    read_s = lambda l, span: fc[l, members, span, :]
    read_b = lambda l, span: bc[l, span, :]
    read_q = lambda l, span: qc[l, span, :]

    pl.semaphore_wait(barrier, total - 1)
    lon_a = [remote(send_al, recv_ah, lon_low), remote(send_ah, recv_al, lon_high)]
    lon_start(lon_a)
    lon_s = lon_field(fc, (members,))
    lon_start(lon_s)
    pack_member(own, lon_cells)
    lat_a = Lat(pack_l.at[:, own, :], pack_h.at[:, own, :], recv_pl.at[:, own, :], recv_ph.at[:, own, :])
    lat_a.start()

    idx, val_w = i_ref[...], w_ref[...]
    n_obs = idx.shape[1]
    row, lane = idx // lat_cells, idx % lat_cells
    at_row = (lax.broadcasted_iota(jnp.int32, (rows, n_obs), 0) == row).astype(F32).astype(BF16)
    at_lane = lax.broadcasted_iota(jnp.int32, (lat_cells, n_obs), 0) == lane
    for val, out in ((val_w, dflat), (val_w * v_ref[...], bflat)):
        acc = None
        for _ in range(3):
            piece_val = val.astype(BF16).astype(F32)
            val = val - piece_val
            placed = jnp.where(at_lane, piece_val, 0.0).astype(BF16)
            term = lax.dot_general(
                at_row, placed, (((1,), (1,)), ((), ())), preferred_element_type=F32
            )
            acc = term if acc is None else acc + term
        out[...] = acc
    for l in range(levels):
        bc[l, :lon_cells, :] = bflat[l * lon_cells : (l + 1) * lon_cells, :]
    lon_b = lon_field(bc, ())
    lon_start(lon_b)
    fill_pack(0, read_s, own, lon_cells)
    fill_pack(1, read_b, own, lon_cells)
    lat_sb = [lat_field(0, fr, (members,), own), lat_field(1, br, (), own)]
    for c in lat_sb:
        c.start()
    zero_edges(fr, (members,))
    zero_edges(br)
    zero_edges(qr)

    def iota(shape, dim):
        return lax.broadcasted_iota(jnp.int32, shape, dim)

    def ext_place(index, cells):
        return jnp.where(index < cells, index, jnp.where(index < cells + RIM, index - cells - RIM, index - RIM))

    def make_matrices(l, _):
        taps = (iota((8, 128), 1) - BAND).astype(F32)

        def weights(kind):
            width = bw_ref[kind, l].astype(F32) + jnp.zeros((1, 1), F32)

            def raw(o):
                return jnp.where(jnp.abs(o) <= width, jnp.exp(-0.5 * (o / (0.5 * width)) ** 2), 0.0)

            norm = jnp.sum(raw(taps)[:1], axis=1, keepdims=True)
            return lambda o: raw(o.astype(F32)) / norm

        def put(ref, where, value):
            hi, lo = split2(value)
            ref[(0, *where)] = hi
            ref[(1, *where)] = lo

        w = weights(0)
        mids = 128 * pl.cdiv(lon_cells + 2 * BAND, 128)
        near = w(iota((lon_cells, mids), 0) - (iota((lon_cells, mids), 1) - BAND))
        near = jnp.where(iota((lon_cells, mids), 1) < lon_cells + 2 * BAND, near, 0.0)
        far = w(iota((mids, ext), 0) - BAND - ext_place(iota((mids, ext), 1), lon_cells))
        put(two_l, (l,), dot3(split2(near), split2(far)))
        put(one_l, (l,), w(iota((lon_cells, ext), 0) - ext_place(iota((lon_cells, ext), 1), lon_cells)))

        w = weights(1)
        mids = 128 * pl.cdiv(lat_cells + 2 * BAND, 128)
        mid = iota((mids, lat_cells), 0) - BAND
        place = lat_at * lat_cells + mid
        keep = (place >= 0) & (place < lat_cells * lat_n) & (mid < lat_cells + BAND)
        back = split2(jnp.where(keep, w(mid - iota((mids, lat_cells), 1)), 0.0))
        out = iota((lat_cells, lat_cells), 1)
        here = iota((lat_cells, mids), 0) - (iota((lat_cells, mids), 1) - BAND)
        put(two_c, (l,), dot3(split2(w(here)), back))
        put(one_c, (l,), w(iota((lat_cells, lat_cells), 0) - out))
        columns = pl.ds(pl.multiple_of(l * lat_cells, lat_cells), lat_cells)
        for side in range(2):
            shift = -RIM if side == 0 else lat_cells
            span = pl.ds(side * lat_cells, lat_cells)

            def rim_at(shape):
                p = iota(shape, 0) - l * RIM
                return p + shift, (p >= 0) & (p < RIM)

            pos, ok = rim_at((lat_cells, mids))
            there = jnp.where(ok, w(pos - (iota((lat_cells, mids), 1) - BAND)), 0.0)
            put(two_r, (span, columns), dot3(split2(there), back))
            pos, ok = rim_at((lat_cells, lat_cells))
            put(one_r, (span, columns), jnp.where(ok, w(pos - out), 0.0))
        return 0

    lax.fori_loop(0, levels, make_matrices, 0)

    lon_wait(lon_a)

    def unpack_member(m, _):
        low, high = recv_al[m].astype(F32), recv_ah[m].astype(F32)
        for l in range(levels):
            fc[l, m, low_rows, :] = low[l * RIM : (l + 1) * RIM]
            fc[l, m, high_rows, :] = high[l * RIM : (l + 1) * RIM]
        return 0

    lax.fori_loop(0, members, unpack_member, 0)
    pack_member(rim, 2 * RIM)
    lat_a2 = Lat(pack_l.at[:, rim, :], pack_h.at[:, rim, :], recv_pl.at[:, rim, :], recv_ph.at[:, rim, :])
    lat_a2.start()
    lon_wait(lon_s)
    lon_wait(lon_b)
    fill_pack(0, read_s, rim, 2 * RIM)
    fill_pack(1, read_b, rim, 2 * RIM)
    lat_sb2 = [lat_field(0, fr, (members,), rim), lat_field(1, br, (), rim)]
    for c in lat_sb2:
        c.start()
    lat_a.wait()
    lat_a2.wait()
    for ref, keep, lanes in ((recv_pl, has_low, low_lanes), (recv_ph, has_high, high_lanes)):
        @pl.when(keep)
        def _():
            def go(m, _):
                fr[m, :, lanes] = ref[m].astype(F32)
                return 0

            lax.fori_loop(0, members, go, 0)

        @pl.when(jnp.logical_not(keep))
        def _():
            def go(m, _):
                fr[m, :, lanes] = jnp.zeros((ext, lat_cells), F32)
                return 0

            lax.fori_loop(0, members, go, 0)

    for c in lat_sb + lat_sb2:
        c.wait()

    def apply(yc, yr, c_mat, r_mat, l_mat, finish):
        def rims(f, _):
            hi, lo = split2(fr[f] * yr[...])
            xrh[f], xrl[f] = hi, lo
            return 0

        lax.fori_loop(0, fields, rims, 0)

        def one_level(l, _):
            columns = pl.ds(pl.multiple_of(l * lat_cells, lat_cells), lat_cells)
            xc = split2((fc[l] * yc[l][None]).reshape(fields * ext, lat_cells))
            xr = (xrh[...].reshape(fields * ext, 2 * lat_cells), xrl[...].reshape(fields * ext, 2 * lat_cells))
            t = dot3(xc, (c_mat[0, l], c_mat[1, l]))
            t = t + dot3(xr, (r_mat[0, :, columns], r_mat[1, :, columns]))
            parts = [
                jnp.concatenate([half[f * ext : (f + 1) * ext] for f in range(fields)], axis=1)
                for half in split2(t)
            ]
            u = dot3((l_mat[0, l], l_mat[1, l]), parts)
            finish(l, [u[:, f * lat_cells : (f + 1) * lat_cells] for f in range(fields)])
            return 0

        lax.fori_loop(0, levels, one_level, 0)

    def finish_cov(l, smoothed):
        acc = fc[l, 0, :lon_cells, :] * smoothed[0]
        for f in range(1, members):
            acc = acc + fc[l, f, :lon_cells, :] * smoothed[f]
        acc = acc * (coef_ens * coef_ens)
        acc = acc + fc[l, members, :lon_cells, :] * smoothed[members] * (coef_static**2 / mem_n)
        part[pl.ds(pl.multiple_of(l * lon_cells, lon_cells), lon_cells), :] = acc

    def piece(owner):
        return pl.ds(pl.multiple_of(owner * chunk, chunk), chunk)

    def mem_copies(src, dst, group):
        out = []
        for j in range(1, mem_n):
            peer = lax.rem(me + j, mem_n)
            copy = pltpu.make_async_remote_copy(
                src_ref=src(peer), dst_ref=dst(j), send_sem=csend.at[group, j],
                recv_sem=crecv.at[group, j], device_id={"mem": peer}, device_id_type=MESH,
            )
            copy.start()
            out.append(copy)
        return out

    def scatter_sum(dst, group):
        copies = mem_copies(lambda peer: part.at[piece(peer)], lambda j: dst.at[j], group)
        acc = part[piece(me), :]
        for j, copy in enumerate(copies):
            copy.wait_recv()
            acc = acc + dst[j + 1]
        for copy in copies:
            copy.wait_send()
        return acc

    def dots_start(left, right, group):
        at = iota((8, lat_cells), 0)
        a = jnp.sum(left, axis=0, keepdims=True)
        b = jnp.sum(right, axis=0, keepdims=True)
        dsend[group] = jnp.where(at == 0, a, jnp.where(at == 1, b, 0.0))
        copies = []
        for step in range(1, total):
            copy = pltpu.make_async_remote_copy(
                src_ref=dsend.at[group], dst_ref=dslots.at[group, step],
                send_sem=dsems.at[group, step], recv_sem=drems.at[group, step],
                device_id=shifted(step), device_id_type=MESH,
            )
            copy.start()
            copies.append(copy)
        return copies

    def dots_end(copies, group):
        for copy in copies:
            copy.wait()
        block = dsend[group] + jnp.sum(dslots[group, 1:], axis=0)
        sums = jnp.sum(block, axis=1, keepdims=True)
        return sums[0:1], sums[1:2]

    apply(bc, br, two_c, two_r, two_l, finish_cov)
    acc = scatter_sum(slots, 0)
    cov[piece(me), :] = acc
    back = mem_copies(lambda peer: cov.at[piece(me)], lambda j: cov.at[piece(me)], 1)
    rhs_mine, diag_mine, cov_mine = bflat[piece(me), :], dflat[piece(me), :], acc
    image_mine = rhs_mine + diag_mine * cov_mine
    dots0 = dots_start(rhs_mine * cov_mine, cov_mine * image_mine, 0)
    for copy in back:
        copy.wait()
    for l in range(levels):
        span = slice(l * lon_cells, (l + 1) * lon_cells)
        qc[l, :lon_cells, :] = bflat[span, :] + dflat[span, :] * cov[span, :]
    lon_q = lon_field(qc, ())
    lon_start(lon_q)
    fill_pack(2, read_q, own, lon_cells)
    lat_q = lat_field(2, qr, (), own)
    lat_q.start()
    lon_wait(lon_q)
    fill_pack(2, read_q, rim, 2 * RIM)
    lat_q2 = lat_field(2, qr, (), rim)
    lat_q2.start()
    lat_q.wait()
    lat_q2.wait()

    apply(qc, qr, two_c, two_r, two_l, finish_cov)
    cov_q = scatter_sum(slots2, 2)
    norm0, curve0 = dots_end(dots0, 0)
    alpha0 = norm0 / curve0
    resid = rhs_mine - alpha0 * image_mine
    cov_r = cov_mine - alpha0 * cov_q
    norm1, curve1 = dots_end(dots_start(resid * cov_r, cov_r * (resid + diag_mine * cov_r), 1), 1)
    beta = norm1 / norm0
    alpha1 = norm1 / (curve1 - beta * norm1 / alpha0)

    def combine(b, q):
        return alpha0 * b + alpha1 * ((b - alpha0 * q) + beta * b)

    for l in range(levels):
        bc[l] = combine(bc[l], qc[l])
    br[...] = combine(br[...], qr[...])

    def finish_control(l, smoothed):
        for f in range(members):
            ens_ref[f, l] = coef_ens * smoothed[f]
        static_ref[l] = coef_static * smoothed[members]

    apply(bc, br, one_c, one_r, one_l, finish_control)


def per_device(anomalies, spread, obs_index, innovation, obs_weight, band_width):
    members = anomalies.shape[0]
    levels, lon_cells, lat_cells = spread.shape
    sizes = tuple(lax.axis_size(a) for a in AXES)
    mem_n, total = sizes[2], math.prod(sizes)
    fields = members + 1
    ext = lon_cells + 2 * RIM
    rows = levels * lon_cells
    chunk = rows // mem_n
    v = pltpu.VMEM
    sem = pltpu.SemaphoreType.DMA
    edge = v((members, levels * RIM, lat_cells), BF16)
    packed = v((members, ext, lat_cells), BF16)
    field = v((levels, ext, lat_cells), F32)
    field_rim = v((ext, 2 * lat_cells), F32)
    mats = [
        v((2, levels, lat_cells, lat_cells), BF16),
        v((2, 2 * lat_cells, levels * lat_cells), BF16),
        v((2, levels, lon_cells, ext), BF16),
    ]
    flat = v((rows, lat_cells), F32)
    scratch = [
        v((levels, fields, ext, lat_cells), F32),
        v((fields, ext, 2 * lat_cells), F32),
        field, field_rim, field, field_rim,
        edge, edge, edge, edge,
        packed, packed, packed, packed,
        v((3, 2, ext, lat_cells), F32),
        v((fields, ext, 2 * lat_cells), BF16),
        v((fields, ext, 2 * lat_cells), BF16),
        *mats, *mats,
        flat, flat, flat, flat,
        v((mem_n, chunk, lat_cells), F32),
        v((mem_n, chunk, lat_cells), F32),
        v((2, total, 8, lat_cells), F32),
        v((2, 8, lat_cells), F32),
        sem((32,)), sem((32,)), sem((3, mem_n)), sem((3, mem_n)), sem((2, total)), sem((2, total)),
    ]
    kernel = functools.partial(fused, dims=(members, levels, lon_cells, lat_cells, sizes))
    return pl.pallas_call(
        kernel,
        out_shape=[
            jax.ShapeDtypeStruct((members, levels, lon_cells, lat_cells), F32),
            jax.ShapeDtypeStruct((levels, lon_cells, lat_cells), F32),
        ],
        in_specs=[VMEM] * 5 + [pl.BlockSpec(memory_space=pltpu.SMEM)],
        out_specs=[VMEM] * 2,
        scratch_shapes=scratch,
        compiler_params=pltpu.CompilerParams(
            collective_id=0, has_side_effects=True, vmem_limit_bytes=60 * 2**20
        ),
    )(
        anomalies, spread, obs_index.reshape(1, -1), obs_weight.reshape(1, -1),
        innovation.reshape(1, -1), band_width,
    )


def solution(mesh):
    return jax.shard_map(
        per_device,
        mesh=mesh,
        in_specs=(
            P("mem", None, "lon", "lat"),
            P(None, "lon", "lat"),
            P("lon", "lat", None),
            P("lon", "lat", None),
            P("lon", "lat", None),
            P(),
        ),
        out_specs=(P("mem", None, "lon", "lat"), P(None, "lon", "lat")),
        check_vma=False,
    )
```

time: 468 us -> 73.5 us (0.16)
  waiting for transfers between devices: 136 us -> 0 us
  local copies, waits for them, and re-layouts: 86.5 us -> 3 us
  blocking collectives: 83.3 us -> 0 us
  Pallas kernels: 0 us -> 69.7 us
  other arithmetic: 50.6 us -> 0 us
  matrix products: 50.2 us -> 0 us
  starting transfers between devices: 36.3 us -> 0 us
  between operations: 21.3 us -> 0.65 us
    psum x2 -> x0, blocking collectives: 83.3 us -> none  [two_products(): lax.psum((local_dot(residual, residual), local_dot(residual, hess_image))...]
    psum x2 -> x0, waiting for transfers between devices: 73.6 us -> none  [forward(): combined = lax.psum(member_part, 'mem') + static_part]
    pallas_call x0 -> x1, Pallas kernels: none -> 69.7 us  [per_device(): pl.pallas_call(kernel, out_shape=[jax.ShapeDtypeStruct((members, levels,...]
    ppermute x20 -> x0, waiting for transfers between devices: 62.1 us -> none  [the longest x10 34.1 us: with_halo(): lax.ppermute(lax.slice_in_dim(block, block.shape[dim] - width, None, axis...]
    dot_general x12 -> x0, matrix products: 50.2 us -> none  [the longest x5 31.9 us: smooth(): jnp.einsum('flja,lij->flia', extended, lon_matrix, precision=lax.Precisio...]
    ppermute x20 -> x0, starting transfers between devices: 36.3 us -> none  [the longest x10 19.2 us: with_halo(): lax.ppermute(lax.slice_in_dim(block, block.shape[dim] - width, None, axis...]
    scatter-add x3 -> x0, other arithmetic: 34.1 us -> none  [the longest x2 22.9 us: observe(): jnp.zeros((cell_count,), jnp.float32).at[clipped].add(obs_term)]
    slice x22 -> x0, local copies, waits for them, and re-layouts: 33.8 us -> none  [the longest x13 22.4 us: with_halo(): lax.slice_in_dim(block, block.shape[dim] - width, None, axis=dim)]
  transfers between devices with their start and end apart: 22 -> 0, of which waited for: 17 -> 0; matrix products, arithmetic and copies ran while one was open for 5% -> 0% of each run, Pallas kernels for 0% -> 0%
where the time goes in v2:
time: 73.5 us; the launch traced here: 73.3 us
  Pallas kernels  69.7 us (95%)
  local copies, waits for them, and re-layouts  3 us (4%)
    pallas_call x1, Pallas kernels, per_device(): pl.pallas_call(kernel, out_shape=[jax.ShapeDtypeStruct((members, levels,...  69.7 us
    unnamed x4, local copies, waits for them, and re-layouts  3 us

profile of v2, /device:TPU:0, one launch (start us, length us, event | category | flops | bytes accessed | tf_op | source)
XLA Modules:
  0.0 73.3 jit_solution(17279859598344413072)
XLA Ops:
  0.6 69.7 %shard_map.77 = (f32[8,4,64,128]{3,2,1,0:T(8,128)}, f32[4,64,128]{2,1,0:T(8,128)}) custom-call(bf16[8,4,64,128]{3,2,1,0:T(8,128)(2,1)} %a_ref.1, f32[4,64,128]{2,1,0:T(8,128)} %s_ref.1, s32[1,2048]{1,0:T(1,128)} %bitcast.3, f32[1,2048]{1,0:T(1,128)} %bitcast.4, f32[1,2048]{1,0:T(1,128)} %bitcast.5, s32[2,4]{1,0:T(2,128)} %bw_ref.1), custom_call_target="tpu_custom_call" | custom-call | tf_op jit(solution)/shard_map/pallas_call | solution.py:485
  70.3 0.0 copy-start
  70.3 2.3 %copy.10 = f32[8,4,64,128]{3,2,1,0:T(8,128)} copy(f32[8,4,64,128]{3,2,1,0:T(8,128)} %get-tuple-element.4) | data formatting | bytes 2097152
  72.6 0.0 copy-done
  72.6 0.7 copy.11
Async XLA Ops:
  70.3 2.4 %copy-start = (f32[4,64,128]{2,1,0:T(8,128)S(1)}, f32[4,64,128]{2,1,0:T(8,128)}, u32[]{:S(2)}) copy-start(f32[4,64,128]{2,1,0:T(8,128)} %get-tuple-element.5) | copy-start | bytes 393220

commit v3 on v2

--- a/solution.py
+++ b/solution.py
@@ -39,7 +39,7 @@
     members, levels, lon_cells, lat_cells, sizes = dims
     (fc, fr, bc, br, qc, qr, send_al, send_ah, recv_al, recv_ah, pack_l, pack_h, recv_pl, recv_ph,
      fpack, xrh, xrl, two_c, two_r, two_l, one_c, one_r, one_l, bflat, dflat, cov, part,
-     slots, slots2, dslots, dsend, send, recv, csend, crecv, dsems, drems) = scratch
+     slots, slots2, dslots, dsend, smoothed_lat, send, recv, csend, crecv, dsems, drems) = scratch
     lon_n, lat_n, mem_n = sizes
     total = lon_n * lat_n * mem_n
     fields = members + 1
@@ -272,6 +272,73 @@
 
     lax.fori_loop(0, levels, make_matrices, 0)
 
+    def lat_part(yc, yr, c_mat, r_mat, l, span, count):
+        columns = pl.ds(pl.multiple_of(l * lat_cells, lat_cells), lat_cells)
+        xc = split2((fc[l, :, span, :] * yc[l, span, :][None]).reshape(fields * count, lat_cells))
+        xr = (
+            xrh[:, span, :].reshape(fields * count, 2 * lat_cells),
+            xrl[:, span, :].reshape(fields * count, 2 * lat_cells),
+        )
+        t = dot3(xc, (c_mat[0, l], c_mat[1, l]))
+        t = t + dot3(xr, (r_mat[0, :, columns], r_mat[1, :, columns]))
+        for h, half in enumerate(split2(t)):
+            smoothed_lat[h, l, span, :] = jnp.concatenate(
+                [half[f * count : (f + 1) * count] for f in range(fields)], axis=1
+            )
+
+    def rim_products(yr, span):
+        def go(f, _):
+            hi, lo = split2(fr[f, span, :] * yr[span, :])
+            xrh[f, span, :], xrl[f, span, :] = hi, lo
+            return 0
+
+        lax.fori_loop(0, fields, go, 0)
+
+    def apply_own(yc, yr, mats):
+        rim_products(yr, own)
+
+        def go(l, _):
+            lat_part(yc, yr, mats[0], mats[1], l, own, lon_cells)
+            return 0
+
+        lax.fori_loop(0, levels, go, 0)
+
+    def apply_rim(yc, yr, mats, finish):
+        rim_products(yr, rim)
+
+        def go(i, _):
+            l = lax.rem(me + 1 + i, levels)
+            lat_part(yc, yr, mats[0], mats[1], l, rim, 2 * RIM)
+            u = dot3((mats[2][0, l], mats[2][1, l]), (smoothed_lat[0, l], smoothed_lat[1, l]))
+            finish(i, l, [u[:, f * lat_cells : (f + 1) * lat_cells] for f in range(fields)])
+            return 0
+
+        lax.fori_loop(0, levels, go, 0)
+
+    def unpack_lat(span, count):
+        for ref, keep, lanes in ((recv_pl, has_low, low_lanes), (recv_ph, has_high, high_lanes)):
+            def go(m, _):
+                fr[m, span, lanes] = ref[m, span, :].astype(F32)
+                return 0
+
+            def clear(m, _):
+                fr[m, span, lanes] = jnp.zeros((count, lat_cells), F32)
+                return 0
+
+            @pl.when(keep)
+            def _():
+                lax.fori_loop(0, members, go, 0)
+
+            @pl.when(jnp.logical_not(keep))
+            def _():
+                lax.fori_loop(0, members, clear, 0)
+
+    lat_a.wait()
+    unpack_lat(own, lon_cells)
+    for c in lat_sb:
+        c.wait()
+    apply_own(bc, br, (two_c, two_r, two_l))
+
     lon_wait(lon_a)
 
     def unpack_member(m, _):
@@ -292,77 +359,45 @@
     lat_sb2 = [lat_field(0, fr, (members,), rim), lat_field(1, br, (), rim)]
     for c in lat_sb2:
         c.start()
-    lat_a.wait()
     lat_a2.wait()
-    for ref, keep, lanes in ((recv_pl, has_low, low_lanes), (recv_ph, has_high, high_lanes)):
-        @pl.when(keep)
-        def _():
-            def go(m, _):
-                fr[m, :, lanes] = ref[m].astype(F32)
-                return 0
-
-            lax.fori_loop(0, members, go, 0)
-
-        @pl.when(jnp.logical_not(keep))
-        def _():
-            def go(m, _):
-                fr[m, :, lanes] = jnp.zeros((ext, lat_cells), F32)
-                return 0
-
-            lax.fori_loop(0, members, go, 0)
-
-    for c in lat_sb + lat_sb2:
+    unpack_lat(rim, 2 * RIM)
+    for c in lat_sb2:
         c.wait()
-
-    def apply(yc, yr, c_mat, r_mat, l_mat, finish):
-        def rims(f, _):
-            hi, lo = split2(fr[f] * yr[...])
-            xrh[f], xrl[f] = hi, lo
-            return 0
-
-        lax.fori_loop(0, fields, rims, 0)
-
-        def one_level(l, _):
-            columns = pl.ds(pl.multiple_of(l * lat_cells, lat_cells), lat_cells)
-            xc = split2((fc[l] * yc[l][None]).reshape(fields * ext, lat_cells))
-            xr = (xrh[...].reshape(fields * ext, 2 * lat_cells), xrl[...].reshape(fields * ext, 2 * lat_cells))
-            t = dot3(xc, (c_mat[0, l], c_mat[1, l]))
-            t = t + dot3(xr, (r_mat[0, :, columns], r_mat[1, :, columns]))
-            parts = [
-                jnp.concatenate([half[f * ext : (f + 1) * ext] for f in range(fields)], axis=1)
-                for half in split2(t)
-            ]
-            u = dot3((l_mat[0, l], l_mat[1, l]), parts)
-            finish(l, [u[:, f * lat_cells : (f + 1) * lat_cells] for f in range(fields)])
-            return 0
-
-        lax.fori_loop(0, levels, one_level, 0)
-
-    def finish_cov(l, smoothed):
-        acc = fc[l, 0, :lon_cells, :] * smoothed[0]
-        for f in range(1, members):
-            acc = acc + fc[l, f, :lon_cells, :] * smoothed[f]
-        acc = acc * (coef_ens * coef_ens)
-        acc = acc + fc[l, members, :lon_cells, :] * smoothed[members] * (coef_static**2 / mem_n)
-        part[pl.ds(pl.multiple_of(l * lon_cells, lon_cells), lon_cells), :] = acc
 
     def piece(owner):
         return pl.ds(pl.multiple_of(owner * chunk, chunk), chunk)
 
-    def mem_copies(src, dst, group):
-        out = []
-        for j in range(1, mem_n):
-            peer = lax.rem(me + j, mem_n)
-            copy = pltpu.make_async_remote_copy(
-                src_ref=src(peer), dst_ref=dst(j), send_sem=csend.at[group, j],
-                recv_sem=crecv.at[group, j], device_id={"mem": peer}, device_id_type=MESH,
-            )
-            copy.start()
-            out.append(copy)
-        return out
+    def mem_copy(src, dst, j, group):
+        return pltpu.make_async_remote_copy(
+            src_ref=src, dst_ref=dst, send_sem=csend.at[group, j], recv_sem=crecv.at[group, j],
+            device_id={"mem": lax.rem(me + j, mem_n)}, device_id_type=MESH,
+        )
+
+    def sum_copy(dst, j, group):
+        return mem_copy(part.at[piece(lax.rem(me + j, mem_n))], dst.at[j], j, group)
+
+    by_level = levels == mem_n
+
+    def finish_cov(dst, group):
+        def finish(i, l, smoothed):
+            acc = fc[l, 0, :lon_cells, :] * smoothed[0]
+            for f in range(1, members):
+                acc = acc + fc[l, f, :lon_cells, :] * smoothed[f]
+            acc = acc * (coef_ens * coef_ens)
+            acc = acc + fc[l, members, :lon_cells, :] * smoothed[members] * (coef_static**2 / mem_n)
+            part[pl.ds(pl.multiple_of(l * lon_cells, lon_cells), lon_cells), :] = acc
+            if by_level:
+                @pl.when(i < mem_n - 1)
+                def _():
+                    sum_copy(dst, i + 1, group).start()
+
+        return finish
 
     def scatter_sum(dst, group):
-        copies = mem_copies(lambda peer: part.at[piece(peer)], lambda j: dst.at[j], group)
+        copies = [sum_copy(dst, j, group) for j in range(1, mem_n)]
+        if not by_level:
+            for copy in copies:
+                copy.start()
         acc = part[piece(me), :]
         for j, copy in enumerate(copies):
             copy.wait_recv()
@@ -372,10 +407,10 @@
         return acc
 
     def dots_start(left, right, group):
-        at = iota((8, lat_cells), 0)
+        at = iota((2, lat_cells), 0)
         a = jnp.sum(left, axis=0, keepdims=True)
         b = jnp.sum(right, axis=0, keepdims=True)
-        dsend[group] = jnp.where(at == 0, a, jnp.where(at == 1, b, 0.0))
+        dsend[group] = jnp.where(at == 0, a, b)
         copies = []
         for step in range(1, total):
             copy = pltpu.make_async_remote_copy(
@@ -394,10 +429,13 @@
         sums = jnp.sum(block, axis=1, keepdims=True)
         return sums[0:1], sums[1:2]
 
-    apply(bc, br, two_c, two_r, two_l, finish_cov)
+    two, one = (two_c, two_r, two_l), (one_c, one_r, one_l)
+    apply_rim(bc, br, two, finish_cov(slots, 0))
     acc = scatter_sum(slots, 0)
     cov[piece(me), :] = acc
-    back = mem_copies(lambda peer: cov.at[piece(me)], lambda j: cov.at[piece(me)], 1)
+    back = [mem_copy(cov.at[piece(me)], cov.at[piece(me)], j, 1) for j in range(1, mem_n)]
+    for copy in back:
+        copy.start()
     rhs_mine, diag_mine, cov_mine = bflat[piece(me), :], dflat[piece(me), :], acc
     image_mine = rhs_mine + diag_mine * cov_mine
     dots0 = dots_start(rhs_mine * cov_mine, cov_mine * image_mine, 0)
@@ -416,9 +454,10 @@
     lat_q2 = lat_field(2, qr, (), rim)
     lat_q2.start()
     lat_q.wait()
+
+    apply_own(qc, qr, two)
     lat_q2.wait()
-
-    apply(qc, qr, two_c, two_r, two_l, finish_cov)
+    apply_rim(qc, qr, two, finish_cov(slots2, 2))
     cov_q = scatter_sum(slots2, 2)
     norm0, curve0 = dots_end(dots0, 0)
     alpha0 = norm0 / curve0
@@ -435,12 +474,13 @@
         bc[l] = combine(bc[l], qc[l])
     br[...] = combine(br[...], qr[...])
 
-    def finish_control(l, smoothed):
+    def finish_control(i, l, smoothed):
         for f in range(members):
             ens_ref[f, l] = coef_ens * smoothed[f]
         static_ref[l] = coef_static * smoothed[members]
 
-    apply(bc, br, one_c, one_r, one_l, finish_control)
+    apply_own(bc, br, one)
+    apply_rim(bc, br, one, finish_control)
 
 
 def per_device(anomalies, spread, obs_index, innovation, obs_weight, band_width):
@@ -477,8 +517,9 @@
         flat, flat, flat, flat,
         v((mem_n, chunk, lat_cells), F32),
         v((mem_n, chunk, lat_cells), F32),
-        v((2, total, 8, lat_cells), F32),
-        v((2, 8, lat_cells), F32),
+        v((2, total, 2, lat_cells), F32),
+        v((2, 2, lat_cells), F32),
+        v((2, levels, ext, fields * lat_cells), BF16),
         sem((32,)), sem((32,)), sem((3, mem_n)), sem((3, mem_n)), sem((2, total)), sem((2, total)),
     ]
     kernel = functools.partial(fused, dims=(members, levels, lon_cells, lat_cells, sizes))

time: 73.5 us -> 66.1 us (0.90)
  Pallas kernels: 69.7 us -> 62.2 us
    pallas_call x1, Pallas kernels: 69.7 us -> 62.2 us  [per_device(): pl.pallas_call(kernel, out_shape=[jax.ShapeDtypeStruct((members, levels,...]
where the time goes in v3:
time: 66.1 us; the launch traced here: 65.9 us
  Pallas kernels  62.2 us (94%)
  local copies, waits for them, and re-layouts  3 us (5%)
    pallas_call x1, Pallas kernels, per_device(): pl.pallas_call(kernel, out_shape=[jax.ShapeDtypeStruct((members, levels,...  62.2 us
    unnamed x4, local copies, waits for them, and re-layouts  3 us

profile of v3, /device:TPU:0, one launch (start us, length us, event | category | flops | bytes accessed | tf_op | source)
XLA Modules:
  0.0 65.9 jit_solution(12518978149945424673)
XLA Ops:
  0.6 62.2 %shard_map.77 = (f32[8,4,64,128]{3,2,1,0:T(8,128)}, f32[4,64,128]{2,1,0:T(8,128)}) custom-call(bf16[8,4,64,128]{3,2,1,0:T(8,128)(2,1)} %a_ref.1, f32[4,64,128]{2,1,0:T(8,128)} %s_ref.1, s32[1,2048]{1,0:T(1,128)} %bitcast.3, f32[1,2048]{1,0:T(1,128)} %bitcast.4, f32[1,2048]{1,0:T(1,128)} %bitcast.5, s32[2,4]{1,0:T(2,128)} %bw_ref.1), custom_call_target="tpu_custom_call" | custom-call | tf_op jit(solution)/shard_map/pallas_call | solution.py:526
  62.9 0.0 copy-start
  62.9 2.3 %copy.10 = f32[8,4,64,128]{3,2,1,0:T(8,128)} copy(f32[8,4,64,128]{3,2,1,0:T(8,128)} %get-tuple-element.4) | data formatting | bytes 2097152
  65.2 0.0 copy-done
  65.2 0.7 copy.11
Async XLA Ops:
  62.9 2.4 %copy-start = (f32[4,64,128]{2,1,0:T(8,128)S(1)}, f32[4,64,128]{2,1,0:T(8,128)}, u32[]{:S(2)}) copy-start(f32[4,64,128]{2,1,0:T(8,128)} %get-tuple-element.5) | copy-start | bytes 393220
